TPU v7x, 32 devices: a whole 2x2x4 slice. The times are simulated.
32 devices in a mesh: gx: 8 (over z, y), gy: 4 (over x, core).
Axes of the slice: x: 2, y: 2, z: 4, core: 2. Of those that a mesh axis runs over, the one named last changes fastest.
Arguments:
- block_input: bfloat16 [960, 8192], P('gx', 'gy'), may hold values from -6 to 6
- attn_gain: float32 [960], P('gx'), may hold values from 0.5 to 1.5
- query_weight: bfloat16 [960, 960], P('gx', 'gy'), may hold values from -2 to 2
- key_weight: bfloat16 [960, 320], P('gx', 'gy'), may hold values from -2 to 2
- value_weight: bfloat16 [960, 320], P('gx', 'gy'), may hold values from -0.1875 to 0.1875
- output_weight: bfloat16 [960, 960], P('gy', 'gx'), may hold values from -0.5 to 0.5
- ffn_gain: float32 [960], P('gx'), may hold values from 0.5 to 1.5
- gate_weight: bfloat16 [960, 2560], P('gx', 'gy'), may hold values from -0.1875 to 0.1875
- up_weight: bfloat16 [960, 2560], P('gx', 'gy'), may hold values from -0.1875 to 0.1875
- down_weight: bfloat16 [2560, 960], P('gy', 'gx'), may hold values from -0.125 to 0.125
- segment_ids: int32 [8, 1024], P('gx'), may hold values from 0 to 7, never falling along the last dimension, each value on 1 to 512 neighbouring positions
- out_cotangent: bfloat16 [960, 8192], P('gx', 'gy'), may hold values from -6 to 6
Outputs:
- block_output: bfloat16 [960, 8192], P('gx', 'gy')
- input_grad: float32 [960, 8192], P('gx', 'gy')
- grad_attngain: float32 [960], P('gx')
- grad_query: float32 [960, 960], P('gx', 'gy')
- grad_key: float32 [960, 320], P('gx', 'gy')
- grad_value: float32 [960, 320], P('gx', 'gy')
- grad_outproj: float32 [960, 960], P('gy', 'gx')
- grad_ffngain: float32 [960], P('gx')
- grad_gate: float32 [960, 2560], P('gx', 'gy')
- grad_up: float32 [960, 2560], P('gx', 'gy')
- grad_down: float32 [2560, 960], P('gy', 'gx')
Inputs may be any that keep to these rules, and one draw needn't show every extreme that they name: `segment_ids`: along each packed sequence the numbers never fall.
All inputs are finite; a program needn't handle non-finite values.
Results may differ from a plain program's by a relative error of at most 0.023.
The roundings to bfloat16 on the way count: a program that leaves them out, or rounds other values in their place, can miss the bound.
Values may be sent and summed in bfloat16 or wider, within the bound.
A program may use at most 256 MiB of HBM per device.

v0:
```python
import math

import jax
import jax.numpy as jnp
from jax import lax
from jax.sharding import PartitionSpec as P

D = 960
QUERY_HEADS = 15
KEY_VALUE_HEADS = 5
HEAD_SIZE = 64
PACKED_LENGTH = 1024


EPS = 1e-05
THETA = 10000.0


def product(left, right):
    return jnp.dot(
        left.astype(jnp.float32),
        right.astype(jnp.float32),
        preferred_element_type=jnp.float32,
        precision=lax.Precision.HIGHEST,
    )


def einsum_full(form, left, right):
    return jnp.einsum(
        form, left.astype(jnp.float32), right.astype(jnp.float32), precision=lax.Precision.HIGHEST
    )


def segment_positions(segments):
    row_index = jnp.arange(segments.shape[1], dtype=jnp.int32)[None, :]
    starts = jnp.concatenate(
        [jnp.ones((segments.shape[0], 1), dtype=jnp.bool_), segments[:, 1:] != segments[:, :-1]],
        axis=1,
    )
    seg_first = lax.cummax(jnp.where(starts, row_index, jnp.zeros_like(row_index)), axis=1)
    return row_index - seg_first


def rope_tables(positions, half_dim):
    frequency = jnp.exp(-math.log(THETA) * jnp.arange(half_dim, dtype=jnp.float32) / half_dim)
    angles = positions.astype(jnp.float32)[:, None] * frequency[None, :]
    return (jnp.cos(angles)[:, None, :], jnp.sin(angles)[:, None, :])


def rotate(values, cos_table, sine_table, rotate_direction):
    n_rows = values.shape[0]
    half_dim = cos_table.shape[-1]
    split_heads = values.reshape(n_rows, -1, 2 * half_dim)
    lower_half = split_heads[..., :half_dim]
    upper_half = split_heads[..., half_dim:]
    new_lower = lower_half * cos_table - rotate_direction * upper_half * sine_table
    new_upper = upper_half * cos_table + rotate_direction * lower_half * sine_table
    return jnp.concatenate([new_lower, new_upper], axis=-1).reshape(n_rows, -1)


def contract_rows(left_rows, right_rows):
    return product(left_rows.T, right_rows)


def width_sum(values):
    return lax.psum(values, "gx")


def norm_forward(values, gain):
    scale = lax.rsqrt(width_sum(jnp.sum(values * values, axis=1)) / D + EPS)
    return (scale, (values * scale[:, None] * gain[None, :]).astype(jnp.bfloat16))


def norm_backward(values, scale, gain, grad_normed):
    weighted = grad_normed * gain[None, :]
    inner = width_sum(jnp.sum(weighted * values, axis=1)) / D
    grad_values = scale[:, None] * weighted - values * (scale * scale * scale * inner)[:, None]
    gain_part = jnp.sum(grad_normed * values * scale[:, None], axis=0)
    return (grad_values, gain_part)


def project_in(local_rows, weight):
    gathered = lax.all_gather(local_rows, "gy", axis=0, tiled=True)
    full_width = lax.all_to_all(gathered, "gx", split_axis=0, concat_axis=1, tiled=True)
    full_weight = lax.all_gather(weight, "gx", axis=0, tiled=True)
    return (gathered, product(full_width, full_weight))


def project_out(local_rows, weight):
    gathered = lax.all_gather(local_rows, "gx", axis=0, tiled=True)
    return (
        gathered,
        lax.psum_scatter(
            product(gathered, weight).astype(jnp.bfloat16), "gy", scatter_dimension=0, tiled=True
        ).astype(jnp.float32),
    )


def to_heads(columns):
    return lax.all_to_all(columns, "gy", split_axis=0, concat_axis=1, tiled=True)


def from_heads(block):
    return lax.all_to_all(block, "gy", split_axis=1, concat_axis=0, tiled=True)


def head_scores(query_per_head, key_per_head, allowed):
    scores = einsum_full("qkgd,ckd->kgqc", query_per_head, key_per_head) * HEAD_SIZE ** (-0.5)
    return jnp.where(allowed[None, None], scores, -jnp.inf)


def shards(
    block_input,
    attn_gain,
    query_weight,
    key_weight,
    value_weight,
    output_weight,
    ffn_gain,
    gate_weight,
    up_weight,
    down_weight,
    segment_ids,
    out_cotangent,
):
    resid_in = block_input.T.astype(jnp.float32)
    cot_local = out_cotangent.T
    scale_one, normed_one = norm_forward(resid_in, attn_gain)
    width_query = query_weight.shape[1]
    width_key = key_weight.shape[1]
    qkv_weight = jnp.concatenate([query_weight, key_weight, value_weight], axis=1)
    normed_one_rows, qkv_sums = project_in(normed_one, qkv_weight)
    qkv_raw = qkv_sums.astype(jnp.bfloat16)
    query_raw = qkv_raw[:, :width_query]
    key_raw = qkv_raw[:, width_query : width_query + width_key]
    value_raw = qkv_raw[:, width_query + width_key :]
    query_block = to_heads(query_raw)
    key_full, value_expanded = (
        lax.all_gather(key_raw, "gy", axis=1, tiled=True),
        lax.all_gather(value_raw, "gy", axis=1, tiled=True),
    )
    block_row_slab = query_block.shape[0]
    query_groups = QUERY_HEADS // KEY_VALUE_HEADS
    query_start = lax.axis_index("gy") * block_row_slab
    seq_start = query_start // PACKED_LENGTH * PACKED_LENGTH
    positions = segment_positions(segment_ids).reshape(-1)
    seg_flat = segment_ids.reshape(-1)
    cos_all, sine_all = rope_tables(positions, HEAD_SIZE // 2)
    cos_query = lax.dynamic_slice_in_dim(cos_all, query_start, block_row_slab, 0)
    sine_query = lax.dynamic_slice_in_dim(sine_all, query_start, block_row_slab, 0)
    key_rotated = rotate(key_full.astype(jnp.float32), cos_all, sine_all, 1.0).astype(jnp.bfloat16)
    query_rotated = rotate(query_block.astype(jnp.float32), cos_query, sine_query, 1.0).astype(
        jnp.bfloat16
    )
    seg_query = lax.dynamic_slice_in_dim(seg_flat, query_start, block_row_slab, 0)
    query_index = query_start - seq_start + jnp.arange(block_row_slab, dtype=jnp.int32)
    key_index = jnp.arange(PACKED_LENGTH, dtype=jnp.int32)
    allowed = (seg_query[:, None] == seg_flat[None, :]) & (
        key_index[None, :] <= query_index[:, None]
    )
    query_per_head = query_rotated.reshape(block_row_slab, KEY_VALUE_HEADS, query_groups, HEAD_SIZE)
    key_per_head = key_rotated.reshape(PACKED_LENGTH, KEY_VALUE_HEADS, HEAD_SIZE)
    value_per_head = value_expanded.reshape(PACKED_LENGTH, KEY_VALUE_HEADS, HEAD_SIZE)
    scores = head_scores(query_per_head, key_per_head, allowed)
    row_top = jnp.max(scores, axis=-1, keepdims=True)
    log_total = row_top + jnp.log(jnp.sum(jnp.exp(scores - row_top), axis=-1, keepdims=True))
    prob_half = jnp.exp(scores - log_total).astype(jnp.bfloat16)
    mixed = einsum_full("kgqc,ckd->qkgd", prob_half, value_per_head)
    attn_block = mixed.reshape(block_row_slab, -1).astype(jnp.bfloat16)
    attn_rows = from_heads(attn_block)
    attn_gathered, attn_sum = project_out(attn_rows, output_weight)
    hidden_in = resid_in + attn_sum
    scale_two, normed_two = norm_forward(hidden_in, ffn_gain)
    width_ff = gate_weight.shape[1]
    gate_up = jnp.concatenate([gate_weight, up_weight], axis=1)
    normed_two_rows, gate_sums = project_in(normed_two, gate_up)
    gate_pre = gate_sums[:, :width_ff]
    up_pre = gate_sums[:, width_ff:]
    hidden = (jax.nn.silu(gate_pre) * up_pre).astype(jnp.bfloat16)
    hidden_gathered, ffn_sum = project_out(hidden, down_weight)
    block_output = (hidden_in + ffn_sum).astype(jnp.bfloat16)
    cot_rows, hidden_grad = project_in(cot_local, down_weight.T)
    grad_down = contract_rows(lax.all_gather(hidden, "gx", axis=0, tiled=True), cot_rows)
    gate_sigmoid = jax.nn.sigmoid(gate_pre)
    gate_back = (
        hidden_grad * up_pre * gate_sigmoid * (1.0 + gate_pre * (1.0 - gate_sigmoid))
    ).astype(jnp.bfloat16)
    up_back = (hidden_grad * gate_pre * gate_sigmoid).astype(jnp.bfloat16)
    gate_up_rows, normed_two_grad = project_out(
        jnp.concatenate([gate_back, up_back], axis=1), gate_up.T
    )
    grad_gate_up = contract_rows(normed_two_rows, gate_up_rows)
    hidden_in_grad, gain_two_part = norm_backward(hidden_in, scale_two, ffn_gain, normed_two_grad)
    hidden_in_grad = hidden_in_grad + cot_local.astype(jnp.float32)
    hidden_in_half = hidden_in_grad.astype(jnp.bfloat16)
    grad_rows, attn_grad = project_in(hidden_in_half, output_weight.T)
    grad_outproj = contract_rows(attn_gathered, grad_rows)
    block_gradient = to_heads(attn_grad.astype(jnp.bfloat16))
    head_gradient = block_gradient.reshape(block_row_slab, KEY_VALUE_HEADS, query_groups, HEAD_SIZE)
    scores = head_scores(query_per_head, key_per_head, allowed)
    prob_full = jnp.exp(scores - log_total)
    prob_half = prob_full.astype(jnp.bfloat16)
    prob_grad = einsum_full("qkgd,ckd->kgqc", head_gradient, value_per_head)
    row_dot = jnp.sum(prob_full * prob_grad, axis=-1, keepdims=True)
    score_grad = (prob_full * (prob_grad - row_dot) * HEAD_SIZE ** (-0.5)).astype(jnp.bfloat16)
    query_grad = einsum_full("kgqc,ckd->qkgd", score_grad, key_per_head).reshape(block_row_slab, -1)
    key_grad = einsum_full("kgqc,qkgd->ckd", score_grad, query_per_head).reshape(PACKED_LENGTH, -1)
    value_grad = einsum_full("kgqc,qkgd->ckd", prob_half, head_gradient).reshape(PACKED_LENGTH, -1)
    query_back = rotate(query_grad, cos_query, sine_query, -1.0).astype(jnp.bfloat16)
    key_grad_all = rotate(key_grad, cos_all, sine_all, -1.0)
    key_back, value_back = (
        lax.psum_scatter(
            key_grad_all.astype(jnp.bfloat16), "gy", scatter_dimension=1, tiled=True
        ).astype(jnp.float32),
        lax.psum_scatter(
            value_grad.astype(jnp.bfloat16), "gy", scatter_dimension=1, tiled=True
        ).astype(jnp.float32),
    )
    query_cols = from_heads(query_back)
    qkv_grad = jnp.concatenate(
        [query_cols, key_back.astype(jnp.bfloat16), value_back.astype(jnp.bfloat16)], axis=1
    )
    qkv_grad_rows, normed_one_grad = project_out(qkv_grad, qkv_weight.T)
    grad_qkv = contract_rows(normed_one_rows, qkv_grad_rows)
    input_grad, gain_one_part = norm_backward(resid_in, scale_one, attn_gain, normed_one_grad)
    input_grad = input_grad + hidden_in_grad
    grad_attngain, grad_ffngain = lax.psum((gain_one_part, gain_two_part), "gy")
    grad_query = grad_qkv[:, :width_query]
    grad_key = grad_qkv[:, width_query : width_query + width_key]
    grad_value = grad_qkv[:, width_query + width_key :]
    grad_gate = grad_gate_up[:, :width_ff]
    grad_up = grad_gate_up[:, width_ff:]
    return (
        block_output.T,
        input_grad.T,
        grad_attngain,
        grad_query,
        grad_key,
        grad_value,
        grad_outproj,
        grad_ffngain,
        grad_gate,
        grad_up,
        grad_down,
    )


def solution(mesh):
    return jax.shard_map(
        shards,
        mesh=mesh,
        in_specs=(
            P("gx", "gy"),
            P("gx"),
            P("gx", "gy"),
            P("gx", "gy"),
            P("gx", "gy"),
            P("gy", "gx"),
            P("gx"),
            P("gx", "gy"),
            P("gx", "gy"),
            P("gy", "gx"),
            P("gx", None),
            P("gx", "gy"),
        ),
        out_specs=(
            P("gx", "gy"),
            P("gx", "gy"),
            P("gx"),
            P("gx", "gy"),
            P("gx", "gy"),
            P("gx", "gy"),
            P("gy", "gx"),
            P("gx"),
            P("gx", "gy"),
            P("gx", "gy"),
            P("gy", "gx"),
        ),
        check_vma=False,
    )
```

profile of v0, /device:TPU:0, one launch (start us, length us, event | category | flops | bytes accessed | tf_op | source)
XLA Modules:
  0.0 1488.9 jit_solution(9215844757252421216)
XLA Ops:
  8.4 23.4 %psum.42 = f32[2048]{0:T(1024)S(1)} all-reduce(f32[2048]{0:T(1024)S(1)} %fusion.35), channel_id=1, replica_groups=mesh['gx'=8,'gy'=4] {'gx'}, use_global_device_ids=true, to_apply=%region_1.0 | all-reduce | flops 2048 | bytes 16384 | tf_op jit(solution)/shard_map/psum | solution.py:66
  33.8 19.2 %all-gather.12.cloned.1.call-done = bf16[8192,120]{0,1:T(8,128)(2,1)} async-done(((bf16[2048,120]{0,1:T(8,128)(2,1)}), bf16[8192,120]{0,1:T(8,128)(2,1)}) %all-gather.12.cloned.1.call-update) | async-done | bytes 1966096 | tf_op jit(solution)/shard_map/all_gather | solution.py:83
  62.7 67.0 %all-gather = bf16[8,120,400]{1,2,0:T(8,128)(2,1)S(1)} all-gather(bf16[1,120,400]{1,2,0:T(8,128)(2,1)S(1)} %fusion.41), channel_id=1, replica_groups=mesh['gx'=8,'gy'=4] {'gx'}, dimensions={0}, use_global_device_ids=true | all-gather | bytes 864000 | tf_op jit(solution)/shard_map/all_gather | solution.py:85
  139.8 12.8 all_gather.46
  195.3 68.4 %all-gather.14.cloned.1.call-done = bf16[8192,240]{0,1:T(8,128)(2,1)} async-done(((bf16[1024,240]{0,1:T(8,128)(2,1)}), bf16[8192,240]{0,1:T(8,128)(2,1)}) %all-gather.14.cloned.1.call-update) | async-done | bytes 3932176 | tf_op jit(solution)/shard_map/all_gather | solution.py:90
  268.1 28.9 %reduce-scatter.7.cloned.1.call-done = bf16[2048,120]{0,1:T(8,128)(2,1)} async-done(((bf16[8192,120]{0,1:T(8,128)(2,1)}), bf16[2048,120]{0,1:T(8,128)(2,1)}) %reduce-scatter.7.cloned.1.call-update) | async-done | bytes 491536 | tf_op jit(solution)/shard_map/reduce_scatter | solution.py:93
  298.3 21.7 %psum.43 = f32[2048]{0:T(1024)S(1)} all-reduce(f32[2048]{0:T(1024)S(1)} %multiply_reduce_fusion), channel_id=1, replica_groups=mesh['gx'=8,'gy'=4] {'gx'}, use_global_device_ids=true, to_apply=%region_8.9 | all-reduce | flops 2048 | bytes 16384 | tf_op jit(solution)/shard_map/psum | solution.py:66
  322.6 17.7 %all-gather.16.cloned.1.call-done = bf16[8192,120]{0,1:T(8,128)(2,1)} async-done(((bf16[2048,120]{0,1:T(8,128)(2,1)}), bf16[8192,120]{0,1:T(8,128)(2,1)}) %all-gather.16.cloned.1.call-update) | async-done | bytes 1966096 | tf_op jit(solution)/shard_map/all_gather | solution.py:83
  349.8 13.8 all-gather.22.cloned.1.call-done
  366.6 38.2 %all-to-all-done.3 = bf16[8,1024,120]{1,2,0:T(8,128)(2,1)} async-done(((bf16[8,1024,120]{1,2,0:T(8,128)(2,1)}), bf16[8,1024,120]{1,2,0:T(8,128)(2,1)}, u32[]{:S(2)}, u32[]{:S(2)}) %all-to-all-start.3) | async-done | bytes 1966112 | tf_op jit(solution)/shard_map/all_to_all | solution.py:84
  409.9 36.0 %all-gather.18.cloned.1.call-done = bf16[960,1280]{1,0:T(8,128)(2,1)} async-done(((bf16[120,1280]{1,0:T(8,128)(2,1)}), bf16[960,1280]{1,0:T(8,128)(2,1)}) %all-gather.18.cloned.1.call-update) | async-done | bytes 2457616 | tf_op jit(solution)/shard_map/all_gather | solution.py:85
  453.5 45.1 %all-gather.24.cloned.1.call-done = bf16[960,640]{1,0:T(8,128)(2,1)} async-done(((bf16[120,640]{1,0:T(8,128)(2,1)}), bf16[960,640]{1,0:T(8,128)(2,1)}) %all-gather.24.cloned.1.call-update) | async-done | bytes 1228816 | tf_op jit(solution)/shard_map/all_gather | solution.py:85
  507.6 400.4 %all-gather.26.cloned.1.call-done = bf16[8192,1280]{1,0:T(8,128)(2,1)} async-done(((bf16[1024,1280]{1,0:T(8,128)(2,1)}), bf16[8192,1280]{1,0:T(8,128)(2,1)}) %all-gather.26.cloned.1.call-update) | async-done | bytes 20971536 | tf_op jit(solution)/shard_map/all_gather | solution.py:90
  908.0 14.8 convolution_convert_fusion.3
  922.9 30.5 %reduce-scatter.11.cloned.1.call-done = bf16[2048,120]{0,1:T(8,128)(2,1)} async-done(((bf16[8192,120]{0,1:T(8,128)(2,1)}), bf16[2048,120]{0,1:T(8,128)(2,1)}) %reduce-scatter.11.cloned.1.call-update) | async-done | bytes 491536 | tf_op jit(solution)/shard_map/reduce_scatter | solution.py:93
  955.4 22.5 %psum.44 = f32[2048]{0:T(1024)} all-reduce(f32[2048]{0:T(1024)S(1)} %get-tuple-element.56), channel_id=1, replica_groups=mesh['gx'=8,'gy'=4] {'gx'}, use_global_device_ids=true, to_apply=%region_12.13 | all-reduce | flops 2048 | bytes 16384 | tf_op jit(solution)/shard_map/psum | solution.py:66
  980.8 18.3 %all-gather.28.cloned.1.call-done = bf16[8192,120]{0,1:T(8,128)(2,1)} async-done(((bf16[2048,120]{0,1:T(8,128)(2,1)}), bf16[8192,120]{0,1:T(8,128)(2,1)}) %all-gather.28.cloned.1.call-update) | async-done | bytes 1966096 | tf_op jit(solution)/shard_map/all_gather | solution.py:83
  1009.2 67.3 %all_gather.55 = bf16[960,240]{1,0:T(8,128)(2,1)} all-gather(bf16[120,240]{1,0:T(8,128)(2,1)} %bitcast.221), channel_id=1, replica_groups=mesh['gx'=8,'gy'=4] {'gx'}, dimensions={0}, use_global_device_ids=true | all-gather | bytes 518400 | tf_op jit(solution)/shard_map/all_gather | solution.py:85
  1078.9 10.9 all_to_all.138
  1106.4 25.3 %fusion.3 = bf16[5,3,256,1024]{2,3,1,0:T(8,128)(2,1)} fusion(f32[5,1024,256,3]{2,1,3,0:T(8,128)} %fusion.54, f32[5,3,256,1024]{2,3,1,0:T(8,128)} %get-tuple-element.86, f32[5,3,256]{2,1,0:T(4,128)S(1)} %log_add_fusion), kind=kOutput, calls=%fused_computation.5 | output fusion | flops 27529984 | bytes 39336960 | tf_op jit(solution)/shard_map/sub | solution.py:205
  1143.5 10.9 all_to_all.139
  1162.5 101.8 %all-gather.30.cloned.1.call-done = bf16[8192,400]{0,1:T(8,128)(2,1)} async-done(((bf16[1024,400]{0,1:T(8,128)(2,1)}), bf16[8192,400]{0,1:T(8,128)(2,1)}) %all-gather.30.cloned.1.call-update) | async-done | bytes 6553616 | tf_op jit(solution)/shard_map/all_gather | solution.py:90
  1269.8 145.3 %all-gather.20.cloned.1.call-done = bf16[8192,640]{1,0:T(8,128)(2,1)} async-done(((bf16[1024,640]{1,0:T(8,128)(2,1)}), bf16[8192,640]{1,0:T(8,128)(2,1)}) %all-gather.20.cloned.1.call-update) | async-done | bytes 10485776 | tf_op jit(solution)/shard_map/all_gather | solution.py:90
  1454.8 20.8 %psum.45 = f32[2048]{0:T(1024)S(1)} all-reduce(f32[2048]{0:T(1024)S(1)} %get-tuple-element.58), channel_id=1, replica_groups=mesh['gx'=8,'gy'=4] {'gx'}, use_global_device_ids=true, to_apply=%region_18.19 | all-reduce | flops 2048 | bytes 16384 | tf_op jit(solution)/shard_map/psum | solution.py:66
  (185 shorter events, 213.3 us)
Async XLA Ops:
  7.2 45.8 %all-gather.12.cloned.1.call-start = ((), (), s32[]{:S(2)}) async-start(), calls=%async_computation.14 | async-start | bytes 2457600 | tf_op jit(solution)/shard_map/all_gather | solution.py:83
  56.0 76.8 %all-to-all-start = ((bf16[8,1024,120]{1,2,0:T(8,128)(2,1)}), bf16[8,1024,120]{1,2,0:T(8,128)(2,1)}, u32[]{:S(2)}, u32[]{:S(2)}) async-start(bf16[8,1024,120]{1,2,0:T(8,128)(2,1)} %bitcast.187), calls=%async_computation | async-start | bytes 3932160 | tf_op jit(solution)/shard_map/all_to_all | solution.py:84
  136.2 24.6 %all-to-all-start.1 = ((bf16[4,256,240]{1,2,0:T(8,128)(2,1)}), bf16[4,256,240]{1,2,0:T(8,128)(2,1)S(1)}, u32[]{:S(2)}, u32[]{:S(2)}) async-start(bf16[4,256,240]{1,2,0:T(8,128)(2,1)} %bitcast.189), calls=%async_computation.1 | async-start | bytes 983040 | tf_op jit(solution)/shard_map/all_to_all | solution.py:100
  139.7 124.0 %all-gather.14.cloned.1.call-start = ((), (), s32[]{:S(2)}) async-start(), calls=%async_computation.15 | async-start | bytes 4423680 | tf_op jit(solution)/shard_map/all_gather | solution.py:90
  195.3 101.8 %reduce-scatter.7.cloned.1.call-start = ((), (), s32[]{:S(2)}) async-start(), calls=%async_computation.16 | async-start | bytes 2457600 | tf_op jit(solution)/shard_map/reduce_scatter | solution.py:93
  267.9 72.4 %all-gather.16.cloned.1.call-start = ((), (), s32[]{:S(2)}) async-start(), calls=%async_computation.17 | async-start | bytes 2457600 | tf_op jit(solution)/shard_map/all_gather | solution.py:83
  322.0 41.6 %all-gather.22.cloned.1.call-start = ((), (), s32[]{:S(2)}) async-start(), calls=%async_computation.21 | async-start | bytes 2457600 | tf_op jit(solution)/shard_map/all_gather | solution.py:83
  343.3 61.5 %all-to-all-start.3 = ((bf16[8,1024,120]{1,2,0:T(8,128)(2,1)}), bf16[8,1024,120]{1,2,0:T(8,128)(2,1)}, u32[]{:S(2)}, u32[]{:S(2)}) async-start(bf16[8,1024,120]{1,2,0:T(8,128)(2,1)} %bitcast.198), calls=%async_computation.4 | async-start | bytes 3932160 | tf_op jit(solution)/shard_map/all_to_all | solution.py:84
  348.9 97.0 %all-gather.18.cloned.1.call-start = ((), (), s32[]{:S(2)}) async-start(), calls=%async_computation.18 | async-start | bytes 2764800 | tf_op jit(solution)/shard_map/all_gather | solution.py:85
  404.8 93.8 %all-to-all-start.4 = ((bf16[8,1024,120]{1,2,0:T(8,128)(2,1)}), bf16[8,1024,120]{1,2,0:T(8,128)(2,1)}, u32[]{:S(2)}, u32[]{:S(2)}) async-start(bf16[8,1024,120]{1,2,0:T(8,128)(2,1)} %bitcast.197), calls=%async_computation.6 | async-start | bytes 3932160 | tf_op jit(solution)/shard_map/all_to_all | solution.py:84
  409.1 89.4 %all-gather.24.cloned.1.call-start = ((), (), s32[]{:S(2)}) async-start(), calls=%async_computation.22 | async-start | bytes 1382400 | tf_op jit(solution)/shard_map/all_gather | solution.py:85
  409.9 498.1 %all-gather.26.cloned.1.call-start = ((), (), s32[]{:S(2)}) async-start(), calls=%async_computation.23 | async-start | bytes 23592960 | tf_op jit(solution)/shard_map/all_gather | solution.py:90
  507.5 400.5 %copy-start.9 = (bf16[120,1280]{1,0:T(8,128)(2,1)S(1)}, bf16[120,1280]{1,0:T(8,128)(2,1)}, u32[]{:S(2)}) copy-start(bf16[120,1280]{1,0:T(8,128)(2,1)} %copy-done.8) | copy-start | bytes 921604
  507.6 445.8 %copy-start.3 = (bf16[2048,120]{0,1:T(8,128)(2,1)S(1)}, bf16[2048,120]{0,1:T(8,128)(2,1)}, u32[]{:S(2)}) copy-start(bf16[2048,120]{0,1:T(8,128)(2,1)} %reduce-scatter.7.cloned.1.call-done) | copy-start | bytes 1474564
  507.6 445.8 %reduce-scatter.11.cloned.1.call-start = ((), (), s32[]{:S(2)}) async-start(), calls=%async_computation.24 | async-start | bytes 2457600 | tf_op jit(solution)/shard_map/reduce_scatter | solution.py:93
  922.9 76.2 %all-gather.28.cloned.1.call-start = ((), (), s32[]{:S(2)}) async-start(), calls=%async_computation.25 | async-start | bytes 2457600 | tf_op jit(solution)/shard_map/all_gather | solution.py:83
  1002.1 74.4 %all-to-all-start.5 = ((bf16[8,1024,120]{1,2,0:T(8,128)(2,1)}), bf16[8,1024,120]{1,2,0:T(8,128)(2,1)}, u32[]{:S(2)}, u32[]{:S(2)}) async-start(bf16[8,1024,120]{1,2,0:T(8,128)(2,1)} %bitcast.199), calls=%async_computation.8 | async-start | bytes 3932160 | tf_op jit(solution)/shard_map/all_to_all | solution.py:84
  1007.6 146.8 %reduce-scatter.15.cloned.1.call-start = ((), (), s32[]{:S(2)}) async-start(), calls=%async_computation.27 | async-start | bytes 819200 | tf_op jit(solution)/shard_map/reduce_scatter | solution.py:215
  1106.4 53.2 %reduce-scatter.13.cloned.1.call-start = ((), (), s32[]{:S(2)}) async-start(), calls=%async_computation.26 | async-start | bytes 819200 | tf_op jit(solution)/shard_map/reduce_scatter | solution.py:212
  1138.6 125.7 %all-gather.30.cloned.1.call-start = ((), (), s32[]{:S(2)}) async-start(), calls=%async_computation.28 | async-start | bytes 7372800 | tf_op jit(solution)/shard_map/all_gather | solution.py:90
  1161.6 253.5 %all-gather.20.cloned.1.call-start = ((), (), s32[]{:S(2)}) async-start(), calls=%async_computation.19 | async-start | bytes 11796480 | tf_op jit(solution)/shard_map/all_gather | solution.py:90
  1162.1 252.9 %copy-start.10 = (bf16[640,120]{0,1:T(8,128)(2,1)S(1)}, bf16[640,120]{0,1:T(8,128)(2,1)}, u32[]{:S(2)}) copy-start(bf16[640,120]{0,1:T(8,128)(2,1)} %param.21) | copy-start | bytes 460804
  1162.2 284.5 %reduce-scatter.17.cloned.1.call-start = ((), (), s32[]{:S(2)}) async-start(), calls=%async_computation.29 | async-start | bytes 2457600 | tf_op jit(solution)/shard_map/reduce_scatter | solution.py:93
  1269.7 209.2 %reduce-scatter.9.cloned.1.call-start = ((), (), s32[]{:S(2)}) async-start(), calls=%async_computation.20 | async-start | bytes 2457600 | tf_op jit(solution)/shard_map/reduce_scatter | solution.py:93
  (26 other events, 727.7 us)
Sparse Core Ops, SparseCore 0:
  33.9 19.0 all-gather.11
  195.4 68.2 all-gather.13
  268.0 28.9 reduce-scatter.6
  322.1 18.1 all-gather.15
  341.7 21.8 all-gather.21
  366.2 79.7 all-gather.17
  448.1 50.4 all-gather.23
  507.7 400.3 all-gather.25
  923.0 30.3 reduce-scatter.10
  981.0 18.1 all-gather.27
  1106.5 20.9 reduce-scatter.14
  1138.7 20.8 reduce-scatter.12
  1162.4 101.8 all-gather.29
  1266.3 148.6 all-gather.19
  1417.5 28.5 reduce-scatter.16
  1448.5 30.3 reduce-scatter.8
where the time goes:
time: 1500 us; the launch traced here: 1490 us
  waiting for transfers between devices  974 us (65%)
  blocking collectives  283 us (19%)
  matrix products  115 us (8%)
  other arithmetic  56.8 us (4%)
  starting transfers between devices  25.7 us (2%)
  local copies, waits for them, and re-layouts  19.8 us (1%)
    all_gather x4, waiting for transfers between devices, project_out(): gathered = lax.all_gather(local_rows, 'gx', axis=0, tiled=True)  716 us
    all_gather x2, blocking collectives, project_in(): full_weight = lax.all_gather(weight, 'gx', axis=0, tiled=True)  134 us
    psum x4, blocking collectives, width_sum(): return lax.psum(values, 'gx')  88.4 us
    all_gather x2, waiting for transfers between devices, project_in(): full_weight = lax.all_gather(weight, 'gx', axis=0, tiled=True)  81.1 us
    dot_general x12, matrix products, product(): jnp.dot(left.astype(jnp.float32), right.astype(jnp.float32), preferred_el...  73.3 us
    all_gather x4, waiting for transfers between devices, project_in(): gathered = lax.all_gather(local_rows, 'gy', axis=0, tiled=True)  69 us
    reduce_scatter x4, waiting for transfers between devices, project_out(): lax.psum_scatter(product(gathered, weight).astype(jnp.bfloat16), 'gy', sc...  62.7 us
    dot_general x6, matrix products, einsum_full(): jnp.einsum(form, left.astype(jnp.float32), right.astype(jnp.float32), pre...  41.8 us
  transfers between devices with their start and end apart: 21, of which 15 were waited for; matrix products, arithmetic and copies ran while one was open for 6% of the time, Pallas kernels for 0%

commit v1 on v0

v1 whole, which is shorter than its diff:
```python
import functools
import math

import jax
import jax.numpy as jnp
from jax import lax
from jax.experimental import pallas as pl
from jax.experimental.pallas import tpu as pltpu
from jax.sharding import PartitionSpec as P

QUERY_HEADS = 15
KEY_VALUE_HEADS = 5
HEAD_SIZE = 64
PACKED_LENGTH = 1024
LONGEST_SEGMENT = 512

EPS = 1e-05
THETA = 10000.0
MESH = pl.DeviceIdType.MESH
F32 = jnp.float32
BF16 = jnp.bfloat16


class Grid:
    def __init__(self, gx, gy):
        self.gx, self.gy = gx, gy
        self.C = 2 if gy % 2 == 0 else 1
        self.X = gy // self.C
        self.Y = self.X if gx % self.X == 0 else 1
        self.Z = gx // self.Y
        self.size = {"z": self.Z, "y": self.Y, "x": self.X}

    def here(self):
        i, j = lax.axis_index("gx"), lax.axis_index("gy")
        return {"z": i // self.Y, "y": i % self.Y, "x": j // self.C, "c": j % self.C}

    def device(self, at):
        return (at["z"] * self.Y + at["y"], at["x"] * self.C + at["c"])


def remote(src, dst, send, recv, device):
    return pltpu.make_async_remote_copy(
        src_ref=src, dst_ref=dst, send_sem=send, recv_sem=recv, device_id=device, device_id_type=MESH
    )


def greet(devices):
    barrier = pltpu.get_barrier_semaphore()
    for device in devices:
        pl.semaphore_signal(barrier, inc=1, device_id=device, device_id_type=MESH)
    pl.semaphore_wait(barrier, len(devices))


def row_peers(n, me):
    return [(d, lax.rem(me + d, n)) for d in range(1, n)]


def line(n, here):
    found = []
    for k in range(1, n):
        if n & (n - 1):
            found.append((lax.rem(here + k, n), lax.rem(here + n - k, n)))
            continue
        place, bit = 0, 1
        while bit < n:
            digit = (here // bit) % 2
            place = place + bit * ((1 - digit) if k & bit else digit)
            bit *= 2
        found.append((place, place))
    return found


def places(n, here):
    return [here] + [origin for _, origin in line(n, here)]


def gather_sites(grid, me, order):
    other = [grid.device({**me, "c": 1 - me["c"]})] if grid.C == 2 else []
    onward = [[grid.device({**me, axis: to}) for to, _ in line(grid.size[axis], me[axis])] for axis in order]
    yield 0, dict(me), sum(onward, []) + other
    for stage, axis in enumerate(order, 1):
        earlier = [dict(me)]
        for done in order[: stage - 1]:
            earlier = [{**e, done: place} for place in places(grid.size[done], me[done]) for e in earlier]
        for _, origin in line(grid.size[axis], me[axis]):
            for e in earlier:
                yield stage, {**e, axis: origin}, sum(onward[stage:], []) + other


def core_sites(grid, me):
    found = [{"c": 1 - me["c"]}]
    for axis in "xyz":
        found = [{**f, axis: place} for place in places(grid.size[axis], me[axis]) for f in found]
    return found


class Lane:
    def __init__(self, order, first, count, width, base, step):
        self.order, self.first, self.count, self.width = order, first, count, width
        self.base, self.step = base, step

    def columns(self, m):
        return pl.ds(pl.multiple_of(self.base + m * self.step, 128), self.width)

    def own_columns(self, m):
        return pl.ds(pl.multiple_of(m * self.width, 128), self.width)

    def at(self, slot, body):
        if isinstance(slot, int):
            if 0 <= slot < self.count:
                body(slot)
        else:
            pl.when((slot >= 0) & (slot < self.count))(lambda: body(slot))

    def at_late(self, slot, body):
        pl.when((slot >= 0) & (slot <= self.count) & (slot != self.count - 1))(lambda: body(slot - slot // self.count))


GROUPS = 4


class Plan:
    def __init__(self, cols, orders):
        self.slots = GROUPS
        tiles = cols // 128 // GROUPS
        most = -(-tiles * 3 // 5)
        least = tiles - most
        self.lanes = [
            Lane(orders[0], 0, GROUPS, most * 128, 0, tiles * 128),
            Lane(orders[1], GROUPS, GROUPS, least * 128, most * 128, tiles * 128),
        ]
        self.chunks = 2 * GROUPS


GATHER_ORDERS = ("zyx", "zxy")
REDUCE_ORDERS = ("xyz", "yxz")


def place_of(grid, piece):
    return piece["x"] * grid.C + piece["c"], piece["z"] * grid.Y + piece["y"]


def other_core(grid, me):
    return grid.device({**me, "c": 1 - me["c"]})


def peers_of(grid, i, j):
    return [(p, j) for _, p in row_peers(grid.gx, i)] + [(i, p) for _, p in row_peers(grid.gy, j)]


class Spread:
    def __init__(self, grid, me, plan, w_ref, out, send, recv):
        self.grid, self.me, self.plan = grid, me, plan
        self.w_ref, self.out, self.send, self.recv = w_ref, out, send, recv
        self.sites = [list(gather_sites(grid, me, lane.order)) for lane in plan.lanes]

    @staticmethod
    def count(grid):
        me = {"z": 0, "y": 0, "x": 0, "c": 0}
        return max(sum(len(sends) for _, _, sends in gather_sites(grid, me, order)) for order in GATHER_ORDERS)

    @staticmethod
    def semaphores(grid, plan):
        return [
            pltpu.SemaphoreType.DMA((Spread.count(grid), plan.chunks)),
            pltpu.SemaphoreType.DMA((grid.gy, grid.gx, plan.chunks)),
        ]

    def stage(self, stage, slot, finish=False):
        for lane, sites in zip(self.plan.lanes, self.sites):
            lane.at(slot, lambda m, lane=lane, sites=sites: self.chunk(lane, sites, stage, m, finish))

    def chunk(self, lane, sites, stage, m, finish):
        number, chunk = 0, lane.first + m
        for at, piece, sends in sites:
            first = number
            number += len(sends)
            if at != stage:
                continue
            j, i = place_of(self.grid, piece)
            land = self.out.at[j, i, :, lane.columns(m)]
            src = self.w_ref.at[:, lane.columns(m)] if at == 0 else land
            arrived = self.recv.at[j, i, chunk]
            if at and not finish:
                remote(land, land, self.send.at[first, chunk], arrived, (0, 0)).wait_recv()
            for n, device in enumerate(sends):
                copy = remote(src, land, self.send.at[first + n, chunk], arrived, device)
                if finish:
                    copy.wait_send()
                else:
                    copy.start()

    def start(self):
        self.stage(0, 0)

    def slot(self, t):
        self.stage(0, t + 1)
        for stage in (1, 2, 3):
            self.stage(stage, t - (stage - 1))
        for lane in self.plan.lanes:
            lane.at(t - 2, functools.partial(self.core, lane))

    def core(self, lane, m):
        if self.grid.C == 2:
            for piece in core_sites(self.grid, self.me):
                j, i = place_of(self.grid, piece)
                land, chunk = self.out.at[j, i, :, lane.columns(m)], lane.first + m
                remote(land, land, self.send.at[0, chunk], self.recv.at[j, i, chunk], (0, 0)).wait_recv()

    def finish(self):
        def end(t, carry):
            for stage in range(4):
                self.stage(stage, t, True)
            return carry

        lax.fori_loop(0, self.plan.slots, end, 0)


class Tokens:
    def __init__(self, grid, i, j, tok, send, recv, local, pairs):
        self.grid, self.i, self.j, self.tok = grid, i, j, tok
        self.send, self.recv, self.local, self.pairs = send, recv, local, pairs

    @staticmethod
    def semaphores(grid, n):
        return [
            pltpu.SemaphoreType.DMA((n, grid.gx - 1)),
            pltpu.SemaphoreType.DMA((n, grid.gx - 1)),
            pltpu.SemaphoreType.DMA((n,)),
        ]

    def of(self, ref, p):
        return ref.at[:, pl.ds(pl.multiple_of(p * self.tok, self.tok), self.tok)]

    def own(self, n):
        pick, land = self.pairs[n]
        return pltpu.make_async_copy(pick(self, self.i), land(self, self.i), self.local.at[n])

    def start(self, n):
        pick, land = self.pairs[n]
        for d, p in row_peers(self.grid.gx, self.i):
            remote(pick(self, p), land(self, self.i), self.send.at[n, d - 1], self.recv.at[n, d - 1], (p, self.j)).start()
        self.own(n).start()

    def finish(self, n):
        pick, land = self.pairs[n]
        for d, p in row_peers(self.grid.gx, self.i):
            sems = self.send.at[n, d - 1], self.recv.at[n, d - 1]
            remote(pick(self, p), land(self, self.i), *sems, (p, self.j)).wait_send()
            back = land(self, lax.rem(self.i + self.grid.gx - d, self.grid.gx))
            remote(back, back, *sems, (p, self.j)).wait_recv()
        self.own(n).wait()


def dot(a, b, contract):
    return lax.dot_general(a, b, ((contract[:1], contract[1:]), ((), ())), preferred_element_type=F32)


def attention_bias(seg_query, seg_window):
    tok, window = seg_query.shape[0], seg_window.shape[1]
    row = lax.broadcasted_iota(jnp.int32, (tok, window), 0) + (window - tok)
    column = lax.broadcasted_iota(jnp.int32, (tok, window), 1)
    return jnp.where((seg_query == seg_window) & (column <= row), 0.0, -jnp.inf).astype(F32)


def head_rows(head):
    return pl.ds(pl.multiple_of(head * HEAD_SIZE, HEAD_SIZE), HEAD_SIZE)


def in_window(win_ref, own_ref, head):
    parts = [win_ref[n, head_rows(head), :] for n in reversed(range(win_ref.shape[0]))]
    return jnp.concatenate(parts + [own_ref[head_rows(head), :]], axis=1)


def probabilities(query, key, bias):
    scores = dot(query, key, (0, 0)) * HEAD_SIZE ** (-0.5) + bias
    raised = jnp.exp(scores - jnp.max(scores, axis=1, keepdims=True))
    return raised * (1.0 / jnp.sum(raised, axis=1, keepdims=True))


def attend(k, kv_heads, groups, q_ref, win_ref, own_ref, bias_ref, o_ref):
    key, value = in_window(win_ref, own_ref, k), in_window(win_ref, own_ref, kv_heads + k)
    for g in range(groups):
        rows = head_rows(k * groups + g)
        prob = probabilities(q_ref[rows, :], key, bias_ref[...]).astype(BF16)
        o_ref[rows, :] = dot(value, prob, (1, 1)).astype(BF16).astype(F32)


def attend_back(k, kv_heads, groups, q_ref, do_ref, win_ref, own_ref, bias_ref, dq_ref, dkv_out, dkv_own):
    key, value = in_window(win_ref, own_ref, k), in_window(win_ref, own_ref, kv_heads + k)
    key_grad = value_grad = None
    for g in range(groups):
        rows = head_rows(k * groups + g)
        query, grad = q_ref[rows, :], do_ref[rows, :]
        prob = probabilities(query, key, bias_ref[...])
        prob_grad = dot(grad, value, (0, 0))
        row_dot = jnp.sum(prob * prob_grad, axis=1, keepdims=True)
        score_grad = (prob * (prob_grad - row_dot) * HEAD_SIZE ** (-0.5)).astype(BF16)
        dq_ref[rows, :] = dot(key, score_grad, (1, 1))
        dk = dot(query, score_grad, (1, 0))
        dv = dot(grad, prob.astype(BF16), (1, 0))
        key_grad = dk if g == 0 else key_grad + dk
        value_grad = dv if g == 0 else value_grad + dv
    tok = q_ref.shape[1]
    for head, grad in ((k, key_grad), (kv_heads + k, value_grad)):
        before = dkv_out.shape[0]
        for n in range(before):
            at = before - 1 - n
            dkv_out[n, head_rows(head), :] = grad[:, at * tok : (at + 1) * tok].astype(BF16)
        dkv_own[head_rows(head), :] = grad[:, before * tok :]


def over(ref, body):
    lead = ref.shape[:-2]
    total = math.prod(lead)

    def one(k, carry):
        place = []
        for n in reversed(lead):
            place.append(k % n)
            k = k // n
        body(tuple(reversed(place)))
        return carry

    if total == 1:
        body((0,) * len(lead))
    else:
        lax.fori_loop(0, total, one, 0)


def add_into(target, source):
    def one(place):
        where = place + (slice(None), slice(None))
        target[where] = target[where] + source[where]

    over(target, one)


DIMS = "xzy"


class Collect:
    def __init__(self, grid, me, plan, acc, from_core, lands, out, c_s, c_r, c_l, l_s, l_r):
        self.grid, self.me, self.plan = grid, me, plan
        self.acc, self.from_core, self.lands, self.out = acc, from_core, lands, out
        self.c_s, self.c_r, self.c_l, self.l_s, self.l_r = c_s, c_r, c_l, l_s, l_r
        self.actions = [self.actions_of(n, lane) for n, lane in enumerate(plan.lanes)]
        self.lags = max(len(actions) for actions in self.actions)

    @staticmethod
    def axes(grid, lane):
        return [axis for axis in lane.order if grid.size[axis] > 1]

    @staticmethod
    def scratch(grid, plan, rows, cols):
        size = (grid.X, grid.Z, grid.Y, rows, cols)
        shapes = [pltpu.VMEM(size, BF16), pltpu.VMEM(size, BF16)]
        for lane in plan.lanes:
            axes = Collect.axes(grid, lane)
            for level, axis in enumerate(axes):
                rest = tuple(grid.size[d] for d in DIMS if d in axes[level + 1 :])
                shapes.append(pltpu.VMEM((grid.size[axis] - 1,) + rest + (rows, lane.count * lane.width), BF16))
        sem = pltpu.SemaphoreType.DMA
        most = max(n - 1 for n in grid.size.values())
        levels = len(shapes) - 2
        return shapes, [sem((grid.X, plan.chunks))] * 3 + [sem((levels, most, plan.chunks))] * 2

    def own_copy(self, x, lane, m, g_ref, columns):
        src, chunk = g_ref.at[x * self.grid.C + self.me["c"], :, :, :, columns], lane.first + m
        return pltpu.make_async_copy(src, self.acc.at[x, :, :, :, lane.columns(m)], self.c_l.at[x, chunk])

    def core_copy(self, x, lane, m, g_ref, columns):
        src, chunk = g_ref.at[x * self.grid.C + 1 - self.me["c"], :, :, :, columns], lane.first + m
        land = self.from_core.at[x, :, :, :, lane.columns(m)]
        return remote(src, land, self.c_s.at[x, chunk], self.c_r.at[x, chunk], other_core(self.grid, self.me))

    def start(self, source):
        self.source = source
        for slot in range(self.plan.slots - 1):
            self.load(slot)

    def load(self, slot):
        for lane in self.plan.lanes:
            ref, at = self.source(lane.base + slot * lane.step)
            for x in range(self.grid.X):
                self.own_copy(x, lane, slot, ref, pl.ds(at, lane.width)).start()
                if self.grid.C == 2:
                    self.core_copy(x, lane, slot, ref, pl.ds(at, lane.width)).start()

    def core(self, lane, m):
        columns = lane.columns(m)
        ref, _ = self.source(0)
        for x in range(self.grid.X):
            self.own_copy(x, lane, m, ref, pl.ds(0, lane.width)).wait()
            if self.grid.C == 2:
                self.core_copy(x, lane, m, ref, pl.ds(0, lane.width)).wait_recv()
                add_into(self.acc.at[x, :, :, :, columns], self.from_core.at[x, :, :, :, columns])

    def level(self, number, lane, level):
        axes = self.axes(self.grid, lane)
        axis = axes[level]
        index = sum(len(self.axes(self.grid, other)) for other in self.plan.lanes[:number]) + level
        free = len(axes) - level - 1

        def pick(t, m):
            place = []
            for d in DIMS:
                if d == axis:
                    place.append(t)
                elif d in axes[level + 1 :]:
                    place.append(slice(None))
                else:
                    place.append(self.me[d] if self.grid.size[d] > 1 else 0)
            return self.acc.at[tuple(place) + (slice(None), lane.columns(m))]

        def land(slot, m):
            return self.lands[index].at[(slot,) + (slice(None),) * (free + 1) + (lane.own_columns(m),)]

        def copies(m):
            for slot, (to, _) in enumerate(line(self.grid.size[axis], self.me[axis])):
                sems = self.l_s.at[index, slot, lane.first + m], self.l_r.at[index, slot, lane.first + m]
                yield slot, remote(pick(to, m), land(slot, m), *sems, self.grid.device({**self.me, axis: to}))

        return self.me[axis], pick, land, copies

    def actions_of(self, number, lane):
        levels = [self.level(number, lane, level) for level in range(len(self.axes(self.grid, lane)))]

        def send(m, copies):
            for _, copy in copies(m):
                copy.start()

        def take(m, p, pick, land, copies, last):
            columns = lane.columns(m)
            if last:
                self.out[:, columns] = pick(p, m)[...].astype(F32)
            for slot, copy in copies(m):
                copy.wait_recv()
                if last:
                    self.out[:, columns] += land(slot, m)[...].astype(F32)
                else:
                    add_into(pick(p, m), land(slot, m))

        actions = [[functools.partial(self.core, lane)]]
        for number, (p, pick, land, copies) in enumerate(levels):
            actions[-1].append(functools.partial(send, copies=copies))
            last = number == len(levels) - 1
            actions.append([functools.partial(take, p=p, pick=pick, land=land, copies=copies, last=last)])
        return actions

    def slot(self, t):
        for lag in range(self.lags):
            for lane, actions in zip(self.plan.lanes, self.actions):
                if lag < len(actions):
                    for action in actions[lag]:
                        lane.at_late(t - lag, action)

    def finish(self):
        def end(t, carry):
            for number, lane in enumerate(self.plan.lanes):

                def body(m, number=number, lane=lane):
                    if self.grid.C == 2:
                        ref, _ = self.source(0)
                        for x in range(self.grid.X):
                            self.core_copy(x, lane, m, ref, pl.ds(0, lane.width)).wait_send()
                    for level in range(len(self.axes(self.grid, lane))):
                        for _, copy in self.level(number, lane, level)[-1](m):
                            copy.wait_send()

                lane.at(t, body)
            return carry

        lax.fori_loop(0, self.plan.slots, end, 0)


class Shift:
    def __init__(self, span, i, j, sign, pick, land, send, recv):
        self.i, self.j, self.q, self.span, self.sign = i, j, i % span, span, sign
        self.pick, self.land, self.send, self.recv = pick, land, send, recv

    def copy(self, n):
        sems = self.send.at[n], self.recv.at[n]
        return remote(self.pick(n), self.land(n), *sems, (self.i + self.sign * (n + 1), self.j))

    def before(self, n):
        return self.q >= n + 1

    def after(self, n):
        return self.q + n + 1 < self.span

    def start(self, slots):
        for n in range(slots):
            pl.when(self.after(n) if self.sign > 0 else self.before(n))(lambda n=n: self.copy(n).start())

    def finish(self, slots, arrived, missing=None):
        for n in range(slots):
            there, goes = (self.before(n), self.after(n)) if self.sign > 0 else (self.after(n), self.before(n))

            def take(n=n):
                self.copy(n).wait_recv()
                arrived(n)

            pl.when(there)(take)
            if missing is not None:
                pl.when(jnp.logical_not(there))(lambda n=n: missing(n))
            pl.when(goes)(lambda n=n: self.copy(n).wait_send())


HBM_SPEC = pl.BlockSpec(memory_space=pl.ANY)
VMEM_SPEC = pl.BlockSpec(memory_space=pltpu.VMEM)


def params(collective_id):
    return pltpu.CompilerParams(
        collective_id=collective_id, has_side_effects=True, vmem_limit_bytes=63 * 1024 * 1024
    )


def column_of(row, size):
    n = row.shape[1]
    same = lax.broadcasted_iota(jnp.int32, (size, n), 0) == lax.broadcasted_iota(jnp.int32, (size, n), 1)
    return jnp.sum(jnp.where(same, row, 0.0), axis=1, keepdims=True)


def row_of(column, size):
    n = column.shape[0]
    same = lax.broadcasted_iota(jnp.int32, (n, size), 0) == lax.broadcasted_iota(jnp.int32, (n, size), 1)
    return jnp.sum(jnp.where(same, column, 0.0), axis=0, keepdims=True)


class Sizes:
    def __init__(self, grid, tok, rows, qc, kc):
        self.grid, self.tok, self.rows, self.qc, self.kc = grid, tok, rows, qc, kc
        self.features = rows * grid.gx
        self.q, self.kv = qc * grid.gy, kc * grid.gy
        self.heads, self.kv_heads = self.q // HEAD_SIZE, self.kv // HEAD_SIZE
        self.groups = self.heads // self.kv_heads
        self.span = PACKED_LENGTH // tok
        self.before = -(-(LONGEST_SEGMENT - 1) // tok)
        self.window = (self.before + 1) * tok
        self.qkv = qc + 2 * kc


def turn(ref, row, cos_table, sine_table, direction):
    half = HEAD_SIZE // 2
    lower = ref[pl.ds(row, half), :]
    upper = ref[pl.ds(pl.multiple_of(row + half, half), half), :]
    if direction > 0:
        lower, upper = lower.astype(BF16).astype(F32), upper.astype(BF16).astype(F32)
    return jnp.concatenate(
        [lower * cos_table - direction * upper * sine_table, upper * cos_table + direction * lower * sine_table], axis=0
    )


def first_kernel(
    sz, plan, width, row_sequences, x_ref, dy_ref, small_ref, w_ref,
    xo, dyo, wo, w_attn, smallo, xn_ref, scale_ref, q_ref, kv_ref, win, o_ref, bias, tables, gains, h_ref, xn2_ref, scale2_ref,
    raw, o_full, t_s, t_r, t_l, k_s, k_r, w_l, w_s, w_r,
):
    grid, tok = sz.grid, sz.tok
    me = grid.here()
    i, j = lax.axis_index("gx"), lax.axis_index("gy")
    greet(peers_of(grid, i, j))
    pairs = [
        (lambda c, p: small_ref, lambda c, p: smallo.at[p]),
        (lambda c, p: c.of(x_ref, p), lambda c, p: xo.at[p]),
        (lambda c, p: c.of(dy_ref, p), lambda c, p: dyo.at[p]),
    ]
    tokens = Tokens(grid, i, j, tok, t_s, t_r, t_l, pairs)
    spread = Spread(grid, me, plan, w_ref, wo, w_s, w_r)
    tokens.start(0)
    tokens.start(1)
    pltpu.make_async_copy(w_ref, wo.at[j, i], w_l.at[0]).start()
    spread.start()
    shift = Shift(sz.span, i, j, 1, lambda n: kv_ref, lambda n: win.at[n], k_s, k_r)
    sequence, q = j * row_sequences + i // sz.span, i % sz.span
    half = HEAD_SIZE // 2

    def norm(parts, scale_out, gain, out):
        total = None
        for k in range(grid.gx):
            value = parts(k)
            part = jnp.sum(value * value, axis=0, keepdims=True)
            total = part if k == 0 else total + part
        scale = lax.rsqrt(total / sz.features + EPS)
        scale_out[...] = scale
        for k in range(grid.gx):
            out[k] = (parts(k) * scale * gains[k, :, gain : gain + 1]).astype(BF16)

    def prepare():
        tokens.finish(0)
        tokens.start(2)

        def segments(place):
            row = smallo[sequence, pl.ds(jnp.maximum(place, 0), 1), :][:, :tok]
            return jnp.where(place >= 0, row, -1.0)

        here = segments(q)
        bias[...] = attention_bias(
            column_of(here, tok), jnp.concatenate([segments(q - n) for n in range(sz.before, 0, -1)] + [here], axis=1)
        )
        first = jnp.zeros((1, tok), F32)
        for n in range(sz.span):
            other = column_of(smallo[sequence, n : n + 1, :][:, :tok], tok)
            first = first + jnp.sum(jnp.where(other < here, 1.0, 0.0), axis=0, keepdims=True)
        positions = (q * tok).astype(F32) + lax.broadcasted_iota(jnp.int32, (1, tok), 1).astype(F32) - first
        frequency = jnp.exp(
            -math.log(THETA) * lax.broadcasted_iota(jnp.int32, (half, 1), 0).astype(F32) / half
        )
        angles = frequency * positions
        tables[0] = jnp.cos(angles)
        tables[1] = jnp.sin(angles)
        for k in range(grid.gx):
            columns = [column_of(smallo[k, sz.span + n : sz.span + n + 1, :][:, :tok], sz.rows) for n in range(2)]
            gains[k] = jnp.concatenate(columns, axis=1)
        tokens.finish(1)
        norm(lambda k: xo[k].astype(F32), scale_ref, 0, xn_ref)

    def project():
        pltpu.make_async_copy(w_ref, wo.at[j, i], w_l.at[0]).wait()
        copy = pltpu.make_async_copy(wo.at[:, :, :, pl.ds(0, width)], w_attn, w_l.at[0])
        copy.start()
        copy.wait()

        def column(b, carry):
            total = None
            for k in range(grid.gx):
                part = dot(w_attn[b, k][:, : sz.qkv], xn_ref[k], (0, 0))
                total = part if k == 0 else total + part
            for part, at, size in ((0, 0, sz.qc), (sz.qc, sz.q, sz.kc), (sz.qc + sz.kc, sz.q + sz.kv, sz.kc)):
                raw[pl.ds(pl.multiple_of(at + b * size, 8), size), :] = total[part : part + size]
            return carry

        lax.fori_loop(0, grid.gy, column, 0)

        def key(k, carry):
            kv_ref[head_rows(k), :] = turn(raw, pl.multiple_of(sz.q + k * HEAD_SIZE, HEAD_SIZE), tables[0], tables[1], 1).astype(BF16)
            kv_ref[head_rows(sz.kv_heads + k), :] = raw[head_rows(sz.heads + sz.kv_heads + k), :].astype(BF16)
            return carry

        lax.fori_loop(0, sz.kv_heads, key, 0)
        shift.start(sz.before)

        def query(k, carry):
            q_ref[head_rows(k), :] = turn(raw, pl.multiple_of(k * HEAD_SIZE, HEAD_SIZE), tables[0], tables[1], 1).astype(BF16)
            return carry

        lax.fori_loop(0, sz.heads, query, 0)

    def zero(n):
        win[n] = jnp.zeros(win.shape[1:], BF16)

    def mix():
        def block(k, carry):
            total = xo[k].astype(F32)
            for b in range(grid.gy):
                mixed = o_full[pl.ds(b * sz.qc, sz.qc), :].astype(BF16)
                total = total + dot(w_attn[b, k][:, sz.qkv : sz.qkv + sz.qc], mixed, (1, 0))
            h_ref[k] = total
            return carry

        lax.fori_loop(0, grid.gx, block, 0)
        norm(lambda k: h_ref[k], scale2_ref, 1, xn2_ref)
        o_ref[...] = o_full[...].astype(BF16)

    each = -(-sz.kv_heads // 2)

    def slot(t, carry):
        spread.slot(t)
        pl.when(t == 0)(prepare)
        pl.when(t == 2)(project)
        pl.when(t == 3)(lambda: shift.finish(sz.before, lambda n: None, zero))

        @pl.when((t == 3) | (t == 4))
        def _():
            def one(k, carry):
                attend(k, sz.kv_heads, sz.groups, q_ref, win, kv_ref, bias, o_full)
                return carry

            lax.fori_loop((t - 3) * each, jnp.minimum((t - 2) * each, sz.kv_heads), one, 0)

        pl.when(t == 5)(mix)
        return carry

    lax.fori_loop(0, plan.slots + 2, slot, 0)
    spread.finish()
    tokens.finish(2)


def first_half(sz, row_sequences, x, dy, small, w):
    grid, tok = sz.grid, sz.tok
    rows, cols = w.shape
    width = cols // GROUPS
    plan = Plan(cols, GATHER_ORDERS)
    parts = (grid.gx, sz.rows, tok)
    outs = [
        (parts, BF16, VMEM_SPEC),
        (parts, BF16, HBM_SPEC),
        ((grid.gy, grid.gx, rows, cols), BF16, HBM_SPEC),
        ((grid.gy, grid.gx, rows, width), BF16, VMEM_SPEC),
        ((grid.gx,) + small.shape, F32, VMEM_SPEC),
        (parts, BF16, VMEM_SPEC),
        ((1, tok), F32, VMEM_SPEC),
        ((sz.q, tok), BF16, VMEM_SPEC),
        ((2 * sz.kv, tok), BF16, VMEM_SPEC),
        ((sz.before, 2 * sz.kv, tok), BF16, VMEM_SPEC),
        ((sz.q, tok), BF16, VMEM_SPEC),
        ((tok, sz.window), F32, VMEM_SPEC),
        ((2, HEAD_SIZE // 2, tok), F32, VMEM_SPEC),
        ((grid.gx, sz.rows, 2), F32, VMEM_SPEC),
        (parts, F32, VMEM_SPEC),
        (parts, BF16, VMEM_SPEC),
        ((1, tok), F32, VMEM_SPEC),
    ]
    return pl.pallas_call(
        functools.partial(first_kernel, sz, plan, width, row_sequences),
        out_shape=[jax.ShapeDtypeStruct(shape, dtype) for shape, dtype, _ in outs],
        in_specs=[VMEM_SPEC] * 4,
        out_specs=[spec for _, _, spec in outs],
        scratch_shapes=[pltpu.VMEM((sz.q + 2 * sz.kv, tok), F32), pltpu.VMEM((sz.q, tok), F32)]
        + Tokens.semaphores(grid, 3)
        + [pltpu.SemaphoreType.DMA((sz.before,))] * 2
        + [pltpu.SemaphoreType.DMA((1,))]
        + Spread.semaphores(grid, plan),
        compiler_params=params(0),
        name="first_half",
    )(x, dy, small, w)


def last_kernel(
    sz, plan, width, both_ref, down_ref, w_attn, xo, xn_ref, scale_ref, q_ref, kv_ref, win, o_ref, bias, tables, gains,
    do_ref, dh_ref, dh_half, bo_ref, gain_two,
    bo, ig, go, gaino,
    dq, dkv_out, dkv_in, dkv, g_attn, dx, ig_parts, gain_parts, gain_in, gain_row, gain_across, acc, from_core, *refs,
):
    lands, (t_s, t_r, t_l, k_s, k_r, g_s, g_r, h_s, h_r, *sems) = refs[:-14], refs[-14:]
    grid, tok = sz.grid, sz.tok
    me = grid.here()
    i, j = lax.axis_index("gx"), lax.axis_index("gy")
    peers, across = row_peers(grid.gx, i), row_peers(grid.gy, j)
    greet(peers_of(grid, i, j))
    collect = Collect(grid, me, plan, acc, from_core, lands, go, *sems)

    def source(first):
        if first < 2 * width:
            return both_ref, first
        return (down_ref, first - 2 * width) if first < 3 * width else (g_attn, first - 3 * width)

    collect.start(source)
    pairs = [
        (lambda c, p: bo_ref.at[p], lambda c, p: c.of(bo, p)),
        (lambda c, p: ig_parts.at[p], lambda c, p: c.of(ig, p)),
    ]
    tokens = Tokens(grid, i, j, tok, t_s, t_r, t_l, pairs)
    shift = Shift(sz.span, i, j, -1, lambda n: dkv_out.at[n], lambda n: dkv_in.at[n], k_s, k_r)

    def column_copies():
        for d, p in peers:
            yield d, remote(gain_parts.at[p], gain_in.at[d - 1], g_s.at[d - 1], g_r.at[d - 1], (p, j))

    def across_copies():
        for d, p in across:
            yield d, remote(gain_row, gain_across.at[d - 1], h_s.at[d - 1], h_r.at[d - 1], (i, p))

    def heads_of(part):
        def one(k, carry):
            attend_back(k, sz.kv_heads, sz.groups, q_ref, do_ref, win, kv_ref, bias, dq, dkv_out, dkv)
            return carry

        each = -(-sz.kv_heads // 3)
        lax.fori_loop(part * each, jnp.minimum((part + 1) * each, sz.kv_heads), one, 0)

    def turn_back(ref, heads):
        def one(k, carry):
            row = pl.multiple_of(k * HEAD_SIZE, HEAD_SIZE)
            ref[head_rows(k), :] = turn(ref, row, tables[0], tables[1], -1)
            return carry

        lax.fori_loop(0, heads, one, 0)

    def back_of(b):
        parts = [
            dq[pl.ds(pl.multiple_of(b * sz.qc, 8), sz.qc), :],
            dkv[pl.ds(pl.multiple_of(b * sz.kc, 8), sz.kc), :],
            dkv[pl.ds(pl.multiple_of(sz.kv + b * sz.kc, 8), sz.kc), :],
        ]
        return jnp.concatenate(parts, axis=0).astype(BF16)

    def block_grads():
        turn_back(dq, sz.heads)

        def arrived(n):
            dkv[...] += dkv_in[n].astype(F32)

        shift.finish(sz.before, arrived)
        turn_back(dkv, sz.kv_heads)

        def column(b, carry):
            back = back_of(b)
            mixed = o_ref[pl.ds(pl.multiple_of(b * sz.qc, 8), sz.qc), :]
            for k in range(grid.gx):
                parts = [dot(xn_ref[k], back, (1, 1)), dot(dh_half[k], mixed, (1, 1))]
                left = width - sz.qkv - sz.qc
                if left:
                    parts.append(jnp.zeros((sz.rows, left), F32))
                g_attn[b, k // grid.Y, k % grid.Y] = jnp.concatenate(parts, axis=1).astype(BF16)
            return carry

        lax.fori_loop(0, grid.gy, column, 0)
        collect.load(plan.slots - 1)

    def input_grads():
        backs = [back_of(b) for b in range(grid.gy)]
        inner = None
        for k in range(grid.gx):
            total = None
            for b in range(grid.gy):
                part = dot(w_attn[b, k][:, : sz.qkv], backs[b], (1, 0))
                total = part if b == 0 else total + part
            dx[k] = total
            value = xo[k].astype(F32)
            part = jnp.sum(total * gains[k, :, 0:1] * value, axis=0, keepdims=True)
            inner = part if k == 0 else inner + part
            gain_parts[k] = gain_two[k]
            gain_parts[k, 0:1, :] = row_of(jnp.sum(total * value * scale_ref[...], axis=1, keepdims=True), 128)
        scale = scale_ref[...]
        inner = scale * scale * scale * inner / sz.features
        for k in range(grid.gx):
            value = xo[k].astype(F32)
            ig_parts[k] = (dh_ref[k] + scale * (dx[k] * gains[k, :, 0:1]) - value * inner).astype(BF16)
        tokens.start(1)
        for _, copy in column_copies():
            copy.start()

    def gain_sums():
        gain_row[...] = gain_parts[i]
        for d, copy in column_copies():
            copy.wait()
            gain_row[...] += gain_in[d - 1]
        for _, copy in across_copies():
            copy.start()

    def slot(t, carry):
        collect.slot(t)
        pl.when(t < 3)(lambda: heads_of(t))

        @pl.when(t == 2)
        def _():
            shift.start(sz.before)
            tokens.start(0)

        pl.when(t == 3)(block_grads)
        pl.when(t == 4)(input_grads)
        pl.when(t == 5)(gain_sums)
        return carry

    lax.fori_loop(0, plan.slots + collect.lags, slot, 0)
    gaino[...] = gain_row[...]
    for d, copy in across_copies():
        copy.wait()
        gaino[...] += gain_across[d - 1]
    tokens.finish(0)
    tokens.finish(1)
    collect.finish()


def last_half(sz, both, down, w_attn, kept, do, dh, dh_half, bo, gain_two):
    grid, tok = sz.grid, sz.tok
    rows, width = w_attn.shape[-2:]
    cols = GROUPS * width
    plan = Plan(cols, REDUCE_ORDERS)
    shapes, sems = Collect.scratch(grid, plan, rows, cols)
    sem = pltpu.SemaphoreType.DMA
    parts = (grid.gx, sz.rows, tok)
    shape = lambda g: g.reshape(grid.gy, grid.Z, grid.Y, rows, -1)
    return pl.pallas_call(
        functools.partial(last_kernel, sz, plan, width),
        out_shape=[
            jax.ShapeDtypeStruct((sz.rows, grid.gx * tok), BF16),
            jax.ShapeDtypeStruct((sz.rows, grid.gx * tok), BF16),
            jax.ShapeDtypeStruct((rows, cols), F32),
            jax.ShapeDtypeStruct((8, 128), F32),
        ],
        in_specs=[HBM_SPEC] * 2 + [VMEM_SPEC] * 16,
        out_specs=[VMEM_SPEC] * 4,
        scratch_shapes=[
            pltpu.VMEM((sz.q, tok), F32),
            pltpu.VMEM((sz.before, 2 * sz.kv, tok), BF16),
            pltpu.VMEM((sz.before, 2 * sz.kv, tok), BF16),
            pltpu.VMEM((2 * sz.kv, tok), F32),
            pltpu.VMEM((grid.gy, grid.Z, grid.Y, rows, width), BF16),
            pltpu.VMEM(parts, F32),
            pltpu.VMEM(parts, BF16),
            pltpu.VMEM((grid.gx, 8, 128), F32),
            pltpu.VMEM((grid.gx - 1, 8, 128), F32),
            pltpu.VMEM((8, 128), F32),
            pltpu.VMEM((grid.gy - 1, 8, 128), F32),
        ]
        + shapes
        + Tokens.semaphores(grid, 2)
        + [sem((sz.before,))] * 2
        + [sem((grid.gx - 1,))] * 2
        + [sem((grid.gy - 1,))] * 2
        + sems,
        compiler_params=params(1),
        name="last_half",
    )(shape(both), shape(down), w_attn, *kept, do, dh, dh_half, bo, gain_two)


def einsum(form, a, b):
    return jnp.einsum(form, a, b, preferred_element_type=F32)


def padded(a, axis, size):
    pads = [(0, 0)] * a.ndim
    pads[axis] = (0, size - a.shape[axis])
    return jnp.pad(a, pads) if size != a.shape[axis] else a


def norm_backward(values, scale, gain, grad):
    weighted = grad * gain[:, None]
    inner = jnp.sum(weighted * values, axis=0) / values.shape[0]
    back = scale * weighted - values * (scale * scale * scale * inner)
    return back, jnp.sum(grad * values * scale, axis=1)


def shards(
    grid,
    block_input,
    attn_gain,
    query_weight,
    key_weight,
    value_weight,
    output_weight,
    ffn_gain,
    gate_weight,
    up_weight,
    down_weight,
    segment_ids,
    out_cotangent,
):
    GX, GY = grid.gx, grid.gy
    rows, row_tokens = block_input.shape
    tok = row_tokens // GX
    sz = Sizes(grid, tok, rows, query_weight.shape[1], key_weight.shape[1])
    fc, features = gate_weight.shape[1], sz.features
    groups = [
        jnp.concatenate([query_weight, key_weight, value_weight, output_weight.T], axis=1), gate_weight, up_weight, down_weight.T
    ]
    width = -(-max(g.shape[1] for g in groups) // 128) * 128
    block = jnp.concatenate([padded(g, 1, width) for g in groups], axis=1)
    small = jnp.concatenate(
        [segment_ids.reshape(sz.span, tok).astype(F32), padded(jnp.stack([attn_gain, ffn_gain]), 1, tok)], axis=0
    )
    small = padded(small, 0, -(-small.shape[0] // 8) * 8)
    (
        x_parts, dy_parts, w_all, w_attn, _, normed_one, scale_one, query, key_value, earlier, mixed, bias, tables, gains,
        hidden_in, normed_two, scale_two,
    ) = first_half(sz, row_tokens // PACKED_LENGTH, block_input, out_cotangent, small, block)
    dy_half = dy_parts.reshape(features, tok)
    w_all = w_all.reshape(GY, features, -1)
    w_gate, w_up, w_down = (w_all[:, :, k * width : k * width + fc] for k in range(1, 4))
    w_out = w_attn.reshape(GY, features, -1)[:, :, sz.qkv : sz.qkv + sz.qc]
    hidden_in, normed_two = hidden_in.reshape(features, tok), normed_two.reshape(features, tok)
    scale_two, gain_two = scale_two[0], gains[:, :, 1].reshape(features)

    gate = einsum("dt,jdf->jtf", normed_two, w_gate)
    up = einsum("dt,jdf->jtf", normed_two, w_up)
    sigmoid = jax.nn.sigmoid(gate)
    hidden = (jax.nn.silu(gate) * up).astype(BF16)
    block_output = (hidden_in + einsum("jdf,jtf->dt", w_down, hidden)).astype(BF16)
    hidden_grad = einsum("dt,jdf->jtf", dy_half, w_down)
    gate_back = (hidden_grad * up * sigmoid * (1.0 + gate * (1.0 - sigmoid))).astype(BF16)
    up_back = (hidden_grad * gate * sigmoid).astype(BF16)
    both_back = jnp.concatenate([padded(gate_back, 2, width), padded(up_back, 2, width)], axis=2)
    grad_both = einsum("dt,jtf->jdf", normed_two, both_back).astype(BF16)
    grad_down = padded(einsum("dt,jtf->jdf", dy_half, hidden).astype(BF16), 2, width)
    normed_two_grad = einsum("jdf,jtf->dt", w_all[:, :, width : 3 * width], both_back)
    hidden_in_grad, gain_two_part = norm_backward(hidden_in, scale_two, gain_two, normed_two_grad)
    hidden_in_grad = hidden_in_grad + dy_half.astype(F32)
    hidden_in_half = hidden_in_grad.astype(BF16)
    head_grad = einsum("jdc,dt->jct", w_out, hidden_in_half).astype(BF16).reshape(-1, tok)

    gain_part = jnp.pad(gain_two_part.reshape(GX, 1, rows), ((0, 0), (1, 6), (0, 128 - rows)))
    parts = (GX, rows, tok)
    block_output, input_grad, grads, gains = last_half(
        sz, grad_both, grad_down, w_attn,
        (x_parts, normed_one, scale_one, query, key_value, earlier, mixed, bias, tables, gains),
        head_grad, hidden_in_grad.reshape(parts), hidden_in_half.reshape(parts), block_output.reshape(parts), gain_part,
    )
    grad_gate, grad_up, grad_down, grad_attn = (grads[:, k * width : (k + 1) * width] for k in range(GROUPS))
    qc, kc = sz.qc, sz.kc
    return (
        block_output,
        input_grad.astype(F32),
        gains[0, :rows],
        grad_attn[:, :qc],
        grad_attn[:, qc : qc + kc],
        grad_attn[:, qc + kc : sz.qkv],
        grad_attn[:, sz.qkv : sz.qkv + qc].T,
        gains[1, :rows],
        grad_gate[:, :fc],
        grad_up[:, :fc],
        grad_down[:, :fc].T,
    )


def solution(mesh):
    grid = Grid(mesh.shape["gx"], mesh.shape["gy"])
    return jax.shard_map(
        functools.partial(shards, grid),
        mesh=mesh,
        in_specs=(
            P("gx", "gy"),
            P("gx"),
            P("gx", "gy"),
            P("gx", "gy"),
            P("gx", "gy"),
            P("gy", "gx"),
            P("gx"),
            P("gx", "gy"),
            P("gx", "gy"),
            P("gy", "gx"),
            P("gx", None),
            P("gx", "gy"),
        ),
        out_specs=(
            P("gx", "gy"),
            P("gx", "gy"),
            P("gx"),
            P("gx", "gy"),
            P("gx", "gy"),
            P("gx", "gy"),
            P("gy", "gx"),
            P("gx"),
            P("gx", "gy"),
            P("gx", "gy"),
            P("gy", "gx"),
        ),
        check_vma=False,
    )
```

time: 1500 us -> 320 us (0.21)
  waiting for transfers between devices: 974 us -> 0 us
  blocking collectives: 283 us -> 0 us
  Pallas kernels: 0 us -> 262 us
  matrix products: 115 us -> 34.7 us
  other arithmetic: 56.8 us -> 5.37 us
  starting transfers between devices: 25.7 us -> 0 us
    all_gather x10 -> x0, waiting for transfers between devices: 866 us -> none  [the longest x4 716 us: project_out(): gathered = lax.all_gather(local_rows, 'gx', axis=0, tiled=True)]
    pallas_call x0 -> x2, Pallas kernels: none -> 262 us  [the longest x1 132 us: last_half(): pl.pallas_call(functools.partial(last_kernel, sz, plan, width), out_shape...]
    all_gather x4 -> x0, blocking collectives: 155 us -> none  [the longest x2 134 us: project_in(): full_weight = lax.all_gather(weight, 'gx', axis=0, tiled=True)]
    psum x5 -> x0, blocking collectives: 95.1 us -> none  [the longest x4 88.4 us: width_sum(): return lax.psum(values, 'gx')]
    dot_general x18 -> x8, matrix products: 115 us -> 34.7 us  [einsum(): return jnp.einsum(form, a, b, preferred_element_type=F32)]
    reduce_scatter x6 -> x0, waiting for transfers between devices: 67.9 us -> none  [the longest x4 62.7 us: project_out(): lax.psum_scatter(product(gathered, weight).astype(jnp.bfloat16), 'gy', sc...]
    all_to_all x5 -> x0, waiting for transfers between devices: 38.2 us -> none  [the longest x4 38.2 us: project_in(): lax.all_to_all(gathered, 'gx', split_axis=0, concat_axis=1, tiled=True)]
    all_to_all x3 -> x0, blocking collectives: 32.6 us -> none  [the longest x2 21.7 us: from_heads(): return lax.all_to_all(block, 'gy', split_axis=1, concat_axis=0, tiled=True)]
  transfers between devices with their start and end apart: 21 -> 0, of which waited for: 15 -> 0; matrix products, arithmetic and copies ran while one was open for 6% -> 0% of each run, Pallas kernels for 0% -> 0%
where the time goes in v1:
time: 320 us; the launch traced here: 319 us
  Pallas kernels  262 us (82%)
  matrix products  34.7 us (11%)
  local copies, waits for them, and re-layouts  15.8 us (5%)
  other arithmetic  5.37 us (2%)
    pallas_call x1, Pallas kernels, last_half(): pl.pallas_call(functools.partial(last_kernel, sz, plan, width), out_shape...  132 us
    pallas_call x1, Pallas kernels, first_half(): pl.pallas_call(functools.partial(first_kernel, sz, plan, width, row_seque...  131 us
    dot_general x8, matrix products, einsum(): return jnp.einsum(form, a, b, preferred_element_type=F32)  34.7 us
    unnamed x35, local copies, waits for them, and re-layouts  6.56 us

profile of v1, /device:TPU:0, one launch (start us, length us, event | category | flops | bytes accessed | tf_op | source)
XLA Modules:
  0.0 319.0 jit_solution(10188767205127238696)
XLA Ops:
  0.6 0.9 copy.34
  1.6 0.8 copy.35
  2.4 0.8 copy.36
  3.3 2.0 concatenate.10.w_ref
  7.3 130.6 %first_half.1 = (bf16[8,120,256]{2,1,0:T(8,128)(2,1)}, bf16[8,120,256]{2,1,0:T(8,128)(2,1)}, bf16[4,8,120,2560]{3,2,1,0:T(8,128)(2,1)}, bf16[4,8,120,640]{3,2,1,...) custom-call(bf16[120,2048]{1,0:T(8,128)(2,1)} %x_ref.1, ...), custom_call_target="tpu_custom_call" | custom-call | tf_op jit(solution)/shard_map/first_half/pallas_call | solution.py:716
  137.9 4.3 %fusion.8 = f32[4,640,256]{2,1,0:T(8,128)S(1)} fusion(bf16[960,256,1]{1,0,2:T(8,128)(2,1)} %bitcast.109, bf16[4,960,2560]{2,1,0:T(8,128)(2,1)} %bitcast.122), kind=kOutput, calls=%fused_computation.9 | convolution fusion | flops 1258291200 | bytes 8028160 | tf_op jit(solution)/shard_map/dt,jdf->jtf/dot_general | solution.py:912
  142.2 4.8 %fusion.4 = f32[4,640,256]{2,1,0:T(8,128)S(1)} fusion(bf16[960,256,1]{1,0,2:T(8,128)(2,1)S(1)} %bitcast.129, bf16[4,960,2560]{2,1,0:T(8,128)(2,1)} %bitcast.123), kind=kOutput, calls=%fused_computation.5 | convolution fusion | flops 1258291200 | bytes 8028160 | tf_op jit(solution)/shard_map/dt,jdf->jtf/dot_general | solution.py:912
  147.2 0.8 slice-done.4
  148.0 4.1 %fusion.19 = (bf16[4,256,640]{1,2,0:T(8,128)(2,1)S(1)}, bf16[4,256,640]{1,2,0:T(8,128)(2,1)}, bf16[4,256,640]{1,2,0:T(8,128)(2,1)}) fusion(f32[4,640,256]{2,1,0:T(8,128)S(1)} %fusion.4, f32[4,640,256]{2,1,0:T(8,128)S(1)} %fusion.8, bf16[960,256,1]{1,0,2:T(8,128)(2,1)S(1)} %bitcast.130, bf16[4,960,2560]{2,1,0:T(8,128)(2,1)S(1)} %bitcast.127), kind=kOutput, calls=%fused_computation.26 | convolution fusion | flops 1268776960 | bytes 14581760 | tf_op jit(solution)/shard_map/dt,jdf->jtf/dot_general | solution.py:912
  152.1 2.2 fusion.35
  154.8 6.4 %bitcast_multiply_fusion.4 = (f32[960,256]{1,0:T(8,128)S(1)}, f32[256]{0:T(256)S(1)}, f32[960,256]{1,0:T(8,128)S(1)}) fusion(f32[8,120,256]{2,1,0:T(8,128)S(1)} %copy-done.3, f32[960]{0:T(1024)S(1)} %mul.89, bf16[4,256,640]{1,2,0:T(8,128)(2,1)} %get-tuple-element.77, bf16[4,256,640]{1,2,0:T(8,128)(2,1)} %get-tuple-element.76, ...), kind=kOutput, calls=%fused_computation.36 | convolution fusion | flops 2522808064 | bytes 15405824 | tf_op jit(solution)/shard_map/jdf,jtf->dt/dot_general | solution.py:912
  161.2 1.2 fusion.45
  162.5 3.9 %fusion.32 = bf16[4,240,256]{2,1,0:T(8,128)(2,1)} fusion(bf16[4,960,640]{2,1,0:T(8,128)(2,1)} %bitcast.107, bf16[960,256]{1,0:T(8,128)(2,1)S(1)} %get-tuple-element.73), kind=kOutput, calls=%fused_computation.34 | convolution fusion | flops 472104960 | bytes 2949120 | tf_op jit(solution)/shard_map/jdc,dt->jct/dot_general | solution.py:912
  167.1 3.8 %convolution_convert_fusion.1 = bf16[4,640,960]{1,2,0:T(8,128)(2,1)} fusion(bf16[4,256,640]{1,2,0:T(8,128)(2,1)S(1)} %get-tuple-element.75, bf16[960,256,1]{1,0,2:T(8,128)(2,1)S(1)} %bitcast.110), kind=kOutput, calls=%fused_computation.11 | convolution fusion | flops 1260748800 | bytes 6717440 | tf_op jit(solution)/shard_map/dt,jtf->jdf/dot_general | solution.py:912
  170.9 5.2 %convolution_convert_fusion = bf16[4,1280,960]{1,2,0:T(8,128)(2,1)} fusion(bf16[960,256,1]{1,0,2:T(8,128)(2,1)S(1)} %bitcast.131, bf16[4,256,640]{1,2,0:T(8,128)(2,1)S(1)} %copy-done.8, bf16[4,256,640]{1,2,0:T(8,128)(2,1)S(1)} %copy-done.7), kind=kOutput, calls=%fused_computation | convolution fusion | flops 2526740480 | bytes 12943360 | tf_op jit(solution)/shard_map/dt,jtf->jdf/dot_general | solution.py:912
  176.1 131.7 %last_half.1 = (bf16[120,2048]{1,0:T(8,128)(2,1)}, bf16[120,2048]{1,0:T(8,128)(2,1)}, f32[120,2560]{1,0:T(8,128)}, f32[8,128]{1,0:T(8,128)}) custom-call(bf16[4,4,2,120,1280]{4,3,2,1,0:T(8,128)(2,1)} %bitcast.106, bf16[4,4,2,120,640]{4,3,2,1,0:T(8,128)(2,1)} %bitcast.105, bf16[4,8,120,640]{3,2,1,0:T(8,128)(2,1)} %get-tuple-element.34.w_attn, ...), custom_call_target="tpu_custom_call" | custom-call | tf_op jit(solution)/shard_map/last_half/pallas_call | solution.py:877
  307.9 2.1 convert_element_type.61
  310.0 2.1 slice_bitcast_fusion
  312.1 1.6 slice_bitcast_fusion.1
  313.7 0.7 copy.44
  314.5 1.1 fusion.47
  315.5 0.7 copy.42
  317.0 1.3 slice_bitcast_fusion.2
  318.2 0.8 copy.51
  (39 shorter events, 4.1 us)
Async XLA Ops:
  137.9 4.3 %copy-start.6 = (bf16[8,120,256]{2,1,0:T(8,128)(2,1)S(1)}, bf16[8,120,256]{2,1,0:T(8,128)(2,1)}, u32[]{:S(2)}) copy-start(bf16[8,120,256]{2,1,0:T(8,128)(2,1)} %get-tuple-element.33) | copy-start | bytes 1474564
  137.9 9.2 %slice-start = ((s8[19660800]{0:T(1024)(128)(4,1)}), s8[4194304]{0:T(1024)(128)(4,1)S(1)}, s32[]{:S(2)}) async-start(s8[19660800]{0:T(1024)(128)(4,1)} %bitcast.125), calls=%async_computation | async-start | bytes 8388608
  137.9 9.2 %slice-start.1 = ((s8[19660800]{0:T(1024)(128)(4,1)}), s8[4194304]{0:T(1024)(128)(4,1)S(1)}, s32[]{:S(2)}) async-start(s8[19660800]{0:T(1024)(128)(4,1)} %bitcast.125), calls=%async_computation.1 | async-start | bytes 8388608
  137.9 9.2 %slice-start.2 = ((s8[19660800]{0:T(1024)(128)(4,1)}), s8[4194304]{0:T(1024)(128)(4,1)S(1)}, s32[]{:S(2)}) async-start(s8[19660800]{0:T(1024)(128)(4,1)} %bitcast.125), calls=%async_computation.2 | async-start | bytes 8388608
  142.2 5.0 %slice-start.3 = ((s8[19660800]{0:T(1024)(128)(4,1)}), s8[4194304]{0:T(1024)(128)(4,1)S(1)}, s32[]{:S(2)}) async-start(s8[19660800]{0:T(1024)(128)(4,1)} %bitcast.125), calls=%async_computation.3 | async-start | bytes 8388608
  142.2 5.8 %slice-start.4 = ((s8[19660800]{0:T(1024)(128)(4,1)}), s8[2883584]{0:T(1024)(128)(4,1)S(1)}, s32[]{:S(2)}) async-start(s8[19660800]{0:T(1024)(128)(4,1)} %bitcast.125), calls=%async_computation.4 | async-start | bytes 5767168
  148.0 4.1 %copy-start.3 = (f32[8,120,256]{2,1,0:T(8,128)S(1)}, f32[8,120,256]{2,1,0:T(8,128)}, u32[]{:S(2)}) copy-start(f32[8,120,256]{2,1,0:T(8,128)} %get-tuple-element.46) | copy-start | bytes 2949124
  152.1 2.2 copy-start
  154.8 6.4 %copy-start.5 = (f32[1,256]{1,0:T(1,128)S(1)}, f32[1,256]{1,0:T(1,128)}, u32[]{:S(2)}) copy-start(f32[1,256]{1,0:T(1,128)} %get-tuple-element.45) | copy-start | bytes 3076
  154.8 6.4 %copy-start.1 = (bf16[8,120,256]{2,1,0:T(8,128)(2,1)S(1)}, bf16[8,120,256]{2,1,0:T(8,128)(2,1)}, u32[]{:S(2)}) copy-start(bf16[8,120,256]{2,1,0:T(8,128)(2,1)} %get-tuple-element.32) | copy-start | bytes 1474564
  162.5 3.9 %copy-start.2 = (bf16[960,256]{1,0:T(8,128)(2,1)}, bf16[960,256]{1,0:T(8,128)(2,1)S(1)}, u32[]{:S(2)}) copy-start(bf16[960,256]{1,0:T(8,128)(2,1)S(1)} %get-tuple-element.73) | copy-start | bytes 1474564
  167.1 3.8 %copy-start.7 = (bf16[4,256,640]{1,2,0:T(8,128)(2,1)S(1)}, bf16[4,256,640]{1,2,0:T(8,128)(2,1)}, u32[]{:S(2)}) copy-start(bf16[4,256,640]{1,2,0:T(8,128)(2,1)} %get-tuple-element.76) | copy-start | bytes 3932164
  167.1 3.8 %copy-start.8 = (bf16[4,256,640]{1,2,0:T(8,128)(2,1)S(1)}, bf16[4,256,640]{1,2,0:T(8,128)(2,1)}, u32[]{:S(2)}) copy-start(bf16[4,256,640]{1,2,0:T(8,128)(2,1)} %get-tuple-element.77) | copy-start | bytes 3932164
  307.9 10.4 %copy-start.4 = (bf16[120,2048]{1,0:T(8,128)(2,1)S(1)}, bf16[120,2048]{1,0:T(8,128)(2,1)}, u32[]{:S(2)}) copy-start(bf16[120,2048]{1,0:T(8,128)(2,1)} %get-tuple-element.102) | copy-start | bytes 1474564

commit v2 on v1

--- a/solution.py
+++ b/solution.py
@@ -94,10 +94,13 @@
     return found
 
 
+GROUPS = 4
+
+
 class Lane:
-    def __init__(self, order, first, count, width, base, step):
-        self.order, self.first, self.count, self.width = order, first, count, width
-        self.base, self.step = base, step
+    def __init__(self, order, first, part, parts, width, base, step):
+        self.order, self.first, self.part, self.parts, self.width = order, first, part, parts, width
+        self.base, self.step, self.count = base, step, GROUPS
 
     def columns(self, m):
         return pl.ds(pl.multiple_of(self.base + m * self.step, 128), self.width)
@@ -106,34 +109,34 @@
         return pl.ds(pl.multiple_of(m * self.width, 128), self.width)
 
     def at(self, slot, body):
+        slots = self.count * self.parts
         if isinstance(slot, int):
-            if 0 <= slot < self.count:
-                body(slot)
-        else:
-            pl.when((slot >= 0) & (slot < self.count))(lambda: body(slot))
-
-    def at_late(self, slot, body):
-        pl.when((slot >= 0) & (slot <= self.count) & (slot != self.count - 1))(lambda: body(slot - slot // self.count))
-
-
-GROUPS = 4
+            if 0 <= slot < slots and slot % self.parts == self.part:
+                body(slot // self.parts)
+            return
+        active = (slot >= 0) & (slot < slots)
+        if self.parts > 1:
+            active = active & (slot % self.parts == self.part)
+        pl.when(active)(lambda: body(slot // self.parts))
 
 
 class Plan:
-    def __init__(self, cols, orders):
-        self.slots = GROUPS
+    def __init__(self, cols, orders, parts):
         tiles = cols // 128 // GROUPS
         most = -(-tiles * 3 // 5)
-        least = tiles - most
-        self.lanes = [
-            Lane(orders[0], 0, GROUPS, most * 128, 0, tiles * 128),
-            Lane(orders[1], GROUPS, GROUPS, least * 128, most * 128, tiles * 128),
-        ]
-        self.chunks = 2 * GROUPS
+        self.lanes, self.parts, self.slots, at = [], parts, GROUPS * parts, 0
+        for part in range(parts):
+            for order, total in zip(orders, (most, tiles - most)):
+                width = total // parts + (part < total % parts)
+                if width:
+                    self.lanes.append(Lane(order, GROUPS * len(self.lanes), part, parts, width * 128, at * 128, tiles * 128))
+                    at += width
+        self.chunks = GROUPS * len(self.lanes)
 
 
 GATHER_ORDERS = ("zyx", "zxy")
 REDUCE_ORDERS = ("xyz", "yxz")
+GATHER_PARTS, REDUCE_PARTS = 1, 1
 
 
 def place_of(grid, piece):
@@ -192,9 +195,10 @@
 
     def start(self):
         self.stage(0, 0)
+        self.stage(0, 1)
 
     def slot(self, t):
-        self.stage(0, t + 1)
+        self.stage(0, t + 2)
         for stage in (1, 2, 3):
             self.stage(stage, t - (stage - 1))
         for lane in self.plan.lanes:
@@ -376,16 +380,20 @@
 
     def start(self, source):
         self.source = source
-        for slot in range(self.plan.slots - 1):
+        for slot in range(self.plan.slots - self.plan.parts):
             self.load(slot)
 
     def load(self, slot):
         for lane in self.plan.lanes:
-            ref, at = self.source(lane.base + slot * lane.step)
-            for x in range(self.grid.X):
-                self.own_copy(x, lane, slot, ref, pl.ds(at, lane.width)).start()
-                if self.grid.C == 2:
-                    self.core_copy(x, lane, slot, ref, pl.ds(at, lane.width)).start()
+
+            def body(m, lane=lane):
+                ref, at = self.source(lane.base + m * lane.step)
+                for x in range(self.grid.X):
+                    self.own_copy(x, lane, m, ref, pl.ds(at, lane.width)).start()
+                    if self.grid.C == 2:
+                        self.core_copy(x, lane, m, ref, pl.ds(at, lane.width)).start()
+
+            lane.at(slot, body)
 
     def core(self, lane, m):
         columns = lane.columns(m)
@@ -448,12 +456,17 @@
             actions.append([functools.partial(take, p=p, pick=pick, land=land, copies=copies, last=last)])
         return actions
 
+    def begin(self, slot):
+        for lane, actions in zip(self.plan.lanes, self.actions):
+            for action in actions[0]:
+                lane.at(slot, action)
+
     def slot(self, t):
-        for lag in range(self.lags):
+        for lag in range(1, self.lags):
             for lane, actions in zip(self.plan.lanes, self.actions):
                 if lag < len(actions):
                     for action in actions[lag]:
-                        lane.at_late(t - lag, action)
+                        lane.at(t - lag, action)
 
     def finish(self):
         def end(t, carry):
@@ -570,9 +583,9 @@
     tokens = Tokens(grid, i, j, tok, t_s, t_r, t_l, pairs)
     spread = Spread(grid, me, plan, w_ref, wo, w_s, w_r)
     tokens.start(0)
+    spread.start()
     tokens.start(1)
     pltpu.make_async_copy(w_ref, wo.at[j, i], w_l.at[0]).start()
-    spread.start()
     shift = Shift(sz.span, i, j, 1, lambda n: kv_ref, lambda n: win.at[n], k_s, k_r)
     sequence, q = j * row_sequences + i // sz.span, i % sz.span
     half = HEAD_SIZE // 2
@@ -590,7 +603,6 @@
 
     def prepare():
         tokens.finish(0)
-        tokens.start(2)
 
         def segments(place):
             row = smallo[sequence, pl.ds(jnp.maximum(place, 0), 1), :][:, :tok]
@@ -614,6 +626,8 @@
         for k in range(grid.gx):
             columns = [column_of(smallo[k, sz.span + n : sz.span + n + 1, :][:, :tok], sz.rows) for n in range(2)]
             gains[k] = jnp.concatenate(columns, axis=1)
+
+    def first_norm():
         tokens.finish(1)
         norm(lambda k: xo[k].astype(F32), scale_ref, 0, xn_ref)
 
@@ -669,6 +683,8 @@
     def slot(t, carry):
         spread.slot(t)
         pl.when(t == 0)(prepare)
+        pl.when(t == 1)(first_norm)
+        pl.when(t == 2)(lambda: tokens.start(2))
         pl.when(t == 2)(project)
         pl.when(t == 3)(lambda: shift.finish(sz.before, lambda n: None, zero))
 
@@ -692,7 +708,7 @@
     grid, tok = sz.grid, sz.tok
     rows, cols = w.shape
     width = cols // GROUPS
-    plan = Plan(cols, GATHER_ORDERS)
+    plan = Plan(cols, GATHER_ORDERS, GATHER_PARTS)
     parts = (grid.gx, sz.rows, tok)
     outs = [
         (parts, BF16, VMEM_SPEC),
@@ -729,10 +745,11 @@
 
 
 def last_kernel(
-    sz, plan, width, both_ref, down_ref, w_attn, xo, xn_ref, scale_ref, q_ref, kv_ref, win, o_ref, bias, tables, gains,
-    do_ref, dh_ref, dh_half, bo_ref, gain_two,
+    sz, plan, width, both_ref, down_ref, w_all, w_attn, xo, xn_ref, scale_ref, q_ref, kv_ref, win, o_ref, bias, tables, gains,
+    back_ref, hidden_ref, h_ref, dy_ref, scale2_ref,
     bo, ig, go, gaino,
-    dq, dkv_out, dkv_in, dkv, g_attn, dx, ig_parts, gain_parts, gain_in, gain_row, gain_across, acc, from_core, *refs,
+    do_ref, dh_ref, dh_half, bo_ref, dq, dkv_out, dkv_in, dkv, g_attn, dx, y_acc, ig_parts, gain_parts, gain_in, gain_row,
+    gain_across, acc, from_core, b_l, *refs,
 ):
     lands, (t_s, t_r, t_l, k_s, k_r, g_s, g_r, h_s, h_r, *sems) = refs[:-14], refs[-14:]
     grid, tok = sz.grid, sz.tok
@@ -768,8 +785,57 @@
             attend_back(k, sz.kv_heads, sz.groups, q_ref, do_ref, win, kv_ref, bias, dq, dkv_out, dkv)
             return carry
 
-        each = -(-sz.kv_heads // 3)
+        each = -(-sz.kv_heads // (2 * plan.parts))
         lax.fori_loop(part * each, jnp.minimum((part + 1) * each, sz.kv_heads), one, 0)
+
+    def feed_back():
+        dx[...] = jnp.zeros_like(dx)
+        y_acc[...] = jnp.zeros_like(y_acc)
+
+        def column(b, carry):
+            copies = [
+                pltpu.make_async_copy(w_all.at[b, :, :, :, pl.ds((n + 1) * width, width)], g_attn.at[n], b_l.at[n])
+                for n in range(3)
+            ]
+            for copy in copies:
+                copy.start()
+            for copy in copies:
+                copy.wait()
+            for k in range(grid.gx):
+                at = k // grid.Y, k % grid.Y
+                dx[k] += dot(g_attn[(0,) + at], back_ref[b, :width, :], (1, 0)) + dot(
+                    g_attn[(1,) + at], back_ref[b, width:, :], (1, 0)
+                )
+                y_acc[k] += dot(g_attn[(2,) + at], hidden_ref[b], (1, 0))
+            return carry
+
+        lax.fori_loop(0, grid.gy, column, 0)
+        scale = scale2_ref[...]
+        inner = None
+        for k in range(grid.gx):
+            part = jnp.sum(dx[k] * gains[k, :, 1:2] * h_ref[k], axis=0, keepdims=True)
+            inner = part if k == 0 else inner + part
+        inner = scale * scale * scale * inner / sz.features
+        for k in range(grid.gx):
+            value, grad = h_ref[k], dx[k]
+            gain_parts[k] = jnp.zeros((8, 128), F32)
+            gain_parts[k, 1:2, :] = row_of(jnp.sum(grad * value * scale, axis=1, keepdims=True), 128)
+            bo_ref[k] = (value + y_acc[k]).astype(BF16)
+            back = dy_ref[k].astype(F32) + (scale * (grad * gains[k, :, 1:2]) - value * inner)
+            dh_ref[k] = back
+            dh_half[k] = back.astype(BF16)
+
+        def heads(b, carry):
+            total = None
+            for k in range(grid.gx):
+                part = dot(w_attn[b, k][:, sz.qkv : sz.qkv + sz.qc], dh_half[k], (0, 0))
+                total = part if k == 0 else total + part
+            dq[pl.ds(pl.multiple_of(b * sz.qc, 8), sz.qc), :] = total
+            return carry
+
+        lax.fori_loop(0, grid.gy, heads, 0)
+        do_ref[...] = dq[...].astype(BF16)
+        tokens.start(0)
 
     def turn_back(ref, heads):
         def one(k, carry):
@@ -797,10 +863,11 @@
         turn_back(dkv, sz.kv_heads)
 
         def column(b, carry):
-            back = back_of(b)
+            back = jnp.transpose(back_of(b).astype(F32)).astype(BF16)
             mixed = o_ref[pl.ds(pl.multiple_of(b * sz.qc, 8), sz.qc), :]
+            mixed = jnp.transpose(mixed.astype(F32)).astype(BF16)
             for k in range(grid.gx):
-                parts = [dot(xn_ref[k], back, (1, 1)), dot(dh_half[k], mixed, (1, 1))]
+                parts = [dot(xn_ref[k], back, (1, 0)), dot(dh_half[k], mixed, (1, 0))]
                 left = width - sz.qkv - sz.qc
                 if left:
                     parts.append(jnp.zeros((sz.rows, left), F32))
@@ -808,7 +875,8 @@
             return carry
 
         lax.fori_loop(0, grid.gy, column, 0)
-        collect.load(plan.slots - 1)
+        for part in range(plan.parts):
+            collect.load(plan.slots - plan.parts + part)
 
     def input_grads():
         backs = [back_of(b) for b in range(grid.gy)]
@@ -822,7 +890,6 @@
             value = xo[k].astype(F32)
             part = jnp.sum(total * gains[k, :, 0:1] * value, axis=0, keepdims=True)
             inner = part if k == 0 else inner + part
-            gain_parts[k] = gain_two[k]
             gain_parts[k, 0:1, :] = row_of(jnp.sum(total * value * scale_ref[...], axis=1, keepdims=True), 128)
         scale = scale_ref[...]
         inner = scale * scale * scale * inner / sz.features
@@ -842,20 +909,24 @@
             copy.start()
 
     def slot(t, carry):
+        pl.when(t == plan.slots - 1)(lambda: collect.begin(t))
         collect.slot(t)
-        pl.when(t < 3)(lambda: heads_of(t))
-
-        @pl.when(t == 2)
+        pl.when(t < plan.slots - 2)(lambda: collect.begin(t + 1))
+        pl.when(t == 0)(feed_back)
+
+        @pl.when(t == 1)
         def _():
+            heads_of(0)
+            heads_of(1)
             shift.start(sz.before)
-            tokens.start(0)
-
-        pl.when(t == 3)(block_grads)
-        pl.when(t == 4)(input_grads)
-        pl.when(t == 5)(gain_sums)
+
+        pl.when(t == 2)(block_grads)
+        pl.when(t == 3)(input_grads)
+        pl.when(t == 4)(gain_sums)
         return carry
 
-    lax.fori_loop(0, plan.slots + collect.lags, slot, 0)
+    collect.begin(0)
+    lax.fori_loop(0, plan.slots + collect.lags - 1, slot, 0)
     gaino[...] = gain_row[...]
     for d, copy in across_copies():
         copy.wait()
@@ -865,11 +936,11 @@
     collect.finish()
 
 
-def last_half(sz, both, down, w_attn, kept, do, dh, dh_half, bo, gain_two):
+def last_half(sz, both, down, w_all, w_attn, kept, back, hidden, h, dy, scale_two):
     grid, tok = sz.grid, sz.tok
     rows, width = w_attn.shape[-2:]
     cols = GROUPS * width
-    plan = Plan(cols, REDUCE_ORDERS)
+    plan = Plan(cols, REDUCE_ORDERS, REDUCE_PARTS)
     shapes, sems = Collect.scratch(grid, plan, rows, cols)
     sem = pltpu.SemaphoreType.DMA
     parts = (grid.gx, sz.rows, tok)
@@ -882,14 +953,19 @@
             jax.ShapeDtypeStruct((rows, cols), F32),
             jax.ShapeDtypeStruct((8, 128), F32),
         ],
-        in_specs=[HBM_SPEC] * 2 + [VMEM_SPEC] * 16,
+        in_specs=[HBM_SPEC] * 3 + [VMEM_SPEC] * 16,
         out_specs=[VMEM_SPEC] * 4,
         scratch_shapes=[
+            pltpu.VMEM((sz.q, tok), BF16),
+            pltpu.VMEM(parts, F32),
+            pltpu.VMEM(parts, BF16),
+            pltpu.VMEM(parts, BF16),
             pltpu.VMEM((sz.q, tok), F32),
             pltpu.VMEM((sz.before, 2 * sz.kv, tok), BF16),
             pltpu.VMEM((sz.before, 2 * sz.kv, tok), BF16),
             pltpu.VMEM((2 * sz.kv, tok), F32),
             pltpu.VMEM((grid.gy, grid.Z, grid.Y, rows, width), BF16),
+            pltpu.VMEM(parts, F32),
             pltpu.VMEM(parts, F32),
             pltpu.VMEM(parts, BF16),
             pltpu.VMEM((grid.gx, 8, 128), F32),
@@ -897,7 +973,9 @@
             pltpu.VMEM((8, 128), F32),
             pltpu.VMEM((grid.gy - 1, 8, 128), F32),
         ]
-        + shapes
+        + shapes[:2]
+        + [sem((3,))]
+        + shapes[2:]
         + Tokens.semaphores(grid, 2)
         + [sem((sz.before,))] * 2
         + [sem((grid.gx - 1,))] * 2
@@ -905,7 +983,7 @@
         + sems,
         compiler_params=params(1),
         name="last_half",
-    )(shape(both), shape(down), w_attn, *kept, do, dh, dh_half, bo, gain_two)
+    )(shape(both), shape(down), shape(w_all), w_attn, *kept, back, hidden, h, dy, scale_two)
 
 
 def einsum(form, a, b):
@@ -916,13 +994,6 @@
     pads = [(0, 0)] * a.ndim
     pads[axis] = (0, size - a.shape[axis])
     return jnp.pad(a, pads) if size != a.shape[axis] else a
-
-
-def norm_backward(values, scale, gain, grad):
-    weighted = grad * gain[:, None]
-    inner = jnp.sum(weighted * values, axis=0) / values.shape[0]
-    back = scale * weighted - values * (scale * scale * scale * inner)
-    return back, jnp.sum(grad * values * scale, axis=1)
 
 
 def shards(
@@ -959,35 +1030,24 @@
         hidden_in, normed_two, scale_two,
     ) = first_half(sz, row_tokens // PACKED_LENGTH, block_input, out_cotangent, small, block)
     dy_half = dy_parts.reshape(features, tok)
-    w_all = w_all.reshape(GY, features, -1)
-    w_gate, w_up, w_down = (w_all[:, :, k * width : k * width + fc] for k in range(1, 4))
-    w_out = w_attn.reshape(GY, features, -1)[:, :, sz.qkv : sz.qkv + sz.qc]
-    hidden_in, normed_two = hidden_in.reshape(features, tok), normed_two.reshape(features, tok)
-    scale_two, gain_two = scale_two[0], gains[:, :, 1].reshape(features)
-
-    gate = einsum("dt,jdf->jtf", normed_two, w_gate)
-    up = einsum("dt,jdf->jtf", normed_two, w_up)
+    w_cols = w_all.reshape(GY, features, -1)
+    w_gate, w_up, w_down = (w_cols[:, :, k * width : k * width + fc] for k in range(1, 4))
+    normed_two = normed_two.reshape(features, tok)
+
+    gate = einsum("jdf,dt->jft", w_gate, normed_two)
+    up = einsum("jdf,dt->jft", w_up, normed_two)
     sigmoid = jax.nn.sigmoid(gate)
-    hidden = (jax.nn.silu(gate) * up).astype(BF16)
-    block_output = (hidden_in + einsum("jdf,jtf->dt", w_down, hidden)).astype(BF16)
-    hidden_grad = einsum("dt,jdf->jtf", dy_half, w_down)
+    hidden = padded((jax.nn.silu(gate) * up).astype(BF16), 1, width)
+    hidden_grad = einsum("jdf,dt->jft", w_down, dy_half)
     gate_back = (hidden_grad * up * sigmoid * (1.0 + gate * (1.0 - sigmoid))).astype(BF16)
     up_back = (hidden_grad * gate * sigmoid).astype(BF16)
-    both_back = jnp.concatenate([padded(gate_back, 2, width), padded(up_back, 2, width)], axis=2)
-    grad_both = einsum("dt,jtf->jdf", normed_two, both_back).astype(BF16)
-    grad_down = padded(einsum("dt,jtf->jdf", dy_half, hidden).astype(BF16), 2, width)
-    normed_two_grad = einsum("jdf,jtf->dt", w_all[:, :, width : 3 * width], both_back)
-    hidden_in_grad, gain_two_part = norm_backward(hidden_in, scale_two, gain_two, normed_two_grad)
-    hidden_in_grad = hidden_in_grad + dy_half.astype(F32)
-    hidden_in_half = hidden_in_grad.astype(BF16)
-    head_grad = einsum("jdc,dt->jct", w_out, hidden_in_half).astype(BF16).reshape(-1, tok)
-
-    gain_part = jnp.pad(gain_two_part.reshape(GX, 1, rows), ((0, 0), (1, 6), (0, 128 - rows)))
-    parts = (GX, rows, tok)
+    both_back = jnp.concatenate([padded(gate_back, 1, width), padded(up_back, 1, width)], axis=1)
+    grad_both = einsum("dt,jft->jdf", normed_two, both_back).astype(BF16)
+    grad_down = einsum("dt,jft->jdf", dy_half, hidden).astype(BF16)
     block_output, input_grad, grads, gains = last_half(
-        sz, grad_both, grad_down, w_attn,
+        sz, grad_both, grad_down, w_all, w_attn,
         (x_parts, normed_one, scale_one, query, key_value, earlier, mixed, bias, tables, gains),
-        head_grad, hidden_in_grad.reshape(parts), hidden_in_half.reshape(parts), block_output.reshape(parts), gain_part,
+        both_back, hidden, hidden_in, dy_parts, scale_two,
     )
     grad_gate, grad_up, grad_down, grad_attn = (grads[:, k * width : (k + 1) * width] for k in range(GROUPS))
     qc, kc = sz.qc, sz.kc

time: 320 us -> 299 us (0.934)
  matrix products: 34.7 us -> 22.3 us
  Pallas kernels: 262 us -> 257 us
  local copies, waits for them, and re-layouts: 15.8 us -> 12.5 us
    dot_general x8 -> x5, matrix products: 34.7 us -> 22.3 us  [einsum(): return jnp.einsum(form, a, b, preferred_element_type=F32)]
    pallas_call x1, Pallas kernels: 131 us -> 120 us  [first_half(): pl.pallas_call(functools.partial(first_kernel, sz, plan, width, row_seque...]
    pallas_call x1, Pallas kernels: 132 us -> 137 us  [last_half(): pl.pallas_call(functools.partial(last_kernel, sz, plan, width), out_shape...]
    unnamed x35 -> x17, local copies, waits for them, and re-layouts: 6.56 us -> 5.55 us
where the time goes in v2:
time: 299 us
  Pallas kernels  257 us (86%)
  matrix products  22.3 us (7%)
  local copies, waits for them, and re-layouts  12.5 us (4%)
  other arithmetic  5.83 us (2%)
    pallas_call x1, Pallas kernels, last_half(): pl.pallas_call(functools.partial(last_kernel, sz, plan, width), out_shape...  137 us
    pallas_call x1, Pallas kernels, first_half(): pl.pallas_call(functools.partial(first_kernel, sz, plan, width, row_seque...  120 us
    dot_general x5, matrix products, einsum(): return jnp.einsum(form, a, b, preferred_element_type=F32)  22.3 us

profile of v2, /device:TPU:0, one launch (start us, length us, event | category | flops | bytes accessed | tf_op | source)
XLA Modules:
  0.0 298.8 jit_solution(13879073547152401823)
XLA Ops:
  0.6 0.7 select_maximum_fusion.1
  1.3 0.7 convert_reduce_fusion
  2.0 0.6 select_maximum_fusion.small_ref
  2.6 0.8 copy.24
  3.5 0.8 copy.25
  4.3 0.9 copy.23
  5.3 2.0 concatenate.10.w_ref
  7.3 119.9 %first_half.1 = (bf16[8,120,256]{2,1,0:T(8,128)(2,1)}, bf16[8,120,256]{2,1,0:T(8,128)(2,1)}, bf16[4,8,120,2560]{3,2,1,0:T(8,128)(2,1)}, bf16[4,8,120,640]{3,2,1,...) custom-call(bf16[120,2048]{1,0:T(8,128)(2,1)} %x_ref.1, ...), custom_call_target="tpu_custom_call" | custom-call | tf_op jit(solution)/shard_map/first_half/pallas_call | solution.py:732
  127.3 4.2 %fusion = f32[4,640,256]{2,1,0:T(8,128)S(1)} fusion(bf16[960,256,1]{1,0,2:T(8,128)(2,1)} %bitcast.44, bf16[4,960,2560]{2,1,0:T(8,128)(2,1)} %bitcast.32), kind=kOutput, calls=%fused_computation.1 | convolution fusion | flops 1258291200 | bytes 8028160 | tf_op jit(solution)/shard_map/jdf,dt->jft/dot_general | solution.py:990
  131.5 4.1 %fusion.4 = f32[4,640,256]{2,1,0:T(8,128)S(1)} fusion(bf16[960,256,1]{1,0,2:T(8,128)(2,1)S(1)} %bitcast.38, bf16[4,960,2560]{2,1,0:T(8,128)(2,1)} %bitcast.33), kind=kOutput, calls=%fused_computation.5 | convolution fusion | flops 1258291200 | bytes 8028160 | tf_op jit(solution)/shard_map/jdf,dt->jft/dot_general | solution.py:990
  135.6 5.0 %multiply_convert_fusion = (bf16[4,640,256]{2,1,0:T(8,128)(2,1)S(1)}, bf16[4,640,256]{2,1,0:T(8,128)(2,1)S(1)}, bf16[4,640,256]{2,1,0:T(8,128)(2,1)S(1)}) fusion(f32[4,640,256]{2,1,0:T(8,128)S(1)} %fusion, f32[4,640,256]{2,1,0:T(8,128)S(1)} %fusion.4, bf16[960,256,1]{1,0,2:T(8,128)(2,1)S(1)} %bitcast.45, bf16[4,960,2560]{2,1,0:T(8,128)(2,1)} %bitcast.34), kind=kOutput, calls=%fused_computation.9 | convolution fusion | flops 1268776960 | bytes 14581760 | tf_op jit(solution)/shard_map/jdf,dt->jft/dot_general | solution.py:990
  140.6 5.4 %convolution_convert_fusion = bf16[4,1280,960]{1,2,0:T(8,128)(2,1)} fusion(bf16[960,256,1]{1,0,2:T(8,128)(2,1)S(1)} %bitcast.46, bf16[4,640,256]{2,1,0:T(8,128)(2,1)S(1)} %get-tuple-element.64, bf16[4,640,256]{2,1,0:T(8,128)(2,1)S(1)} %get-tuple-element.63), kind=kOutput, calls=%fused_computation | convolution fusion | flops 2526740480 | bytes 12943360 | tf_op jit(solution)/shard_map/dt,jft->jdf/dot_general | solution.py:990
  146.0 3.7 %convolution_convert_fusion.1 = bf16[4,640,960]{1,2,0:T(8,128)(2,1)} fusion(bf16[4,640,256]{2,1,0:T(8,128)(2,1)S(1)} %get-tuple-element.62.hidden_ref, bf16[960,256,1]{1,0,2:T(8,128)(2,1)S(1)} %bitcast.39), kind=kOutput, calls=%fused_computation.7 | convolution fusion | flops 1260748800 | bytes 6717440 | tf_op jit(solution)/shard_map/dt,jft->jdf/dot_general | solution.py:990
  149.7 1.6 pad_maximum_fusion.back_ref
  151.3 137.4 %last_half.1 = (bf16[120,2048]{1,0:T(8,128)(2,1)}, bf16[120,2048]{1,0:T(8,128)(2,1)}, f32[120,2560]{1,0:T(8,128)}, f32[8,128]{1,0:T(8,128)}) custom-call(bf16[4,4,2,120,1280]{4,3,2,1,0:T(8,128)(2,1)} %bitcast.37, bf16[4,4,2,120,640]{4,3,2,1,0:T(8,128)(2,1)} %bitcast.36, bf16[4,4,2,120,2560]{4,3,2,1,0:T(8,128)(2,1)} %bitcast.35, ...), custom_call_target="tpu_custom_call" | custom-call | tf_op jit(solution)/shard_map/last_half/pallas_call | solution.py:948
  288.7 2.2 convert_element_type.43
  290.9 1.3 slice_bitcast_fusion.2
  292.2 1.6 slice_bitcast_fusion.1
  293.8 1.1 fusion.6
  294.9 0.7 copy.26
  295.6 0.7 copy.27
  296.3 0.7 copy.28
  297.0 0.9 slice_bitcast_fusion
  298.0 0.8 copy.30
  (11 shorter events, 0.0 us)
Async XLA Ops:
  127.2 4.2 %copy-start.1 = (bf16[8,120,256]{2,1,0:T(8,128)(2,1)S(1)}, bf16[8,120,256]{2,1,0:T(8,128)(2,1)}, u32[]{:S(2)}) copy-start(bf16[8,120,256]{2,1,0:T(8,128)(2,1)} %get-tuple-element.32.dy_ref) | copy-start | bytes 1474564
  131.5 4.1 %copy-start.4 = (bf16[8,120,256]{2,1,0:T(8,128)(2,1)S(1)}, bf16[8,120,256]{2,1,0:T(8,128)(2,1)}, u32[]{:S(2)}) copy-start(bf16[8,120,256]{2,1,0:T(8,128)(2,1)} %get-tuple-element.33) | copy-start | bytes 1474564
  140.6 5.4 %copy-start = (bf16[4,640,256]{2,1,0:T(8,128)(2,1)}, bf16[4,640,256]{2,1,0:T(8,128)(2,1)S(1)}, u32[]{:S(2)}) copy-start(bf16[4,640,256]{2,1,0:T(8,128)(2,1)S(1)} %get-tuple-element.62.hidden_ref) | copy-start | bytes 3932164
  288.7 8.3 %copy-start.2 = (f32[120,2560]{1,0:T(8,128)S(1)}, f32[120,2560]{1,0:T(8,128)}, u32[]{:S(2)}) copy-start(f32[120,2560]{1,0:T(8,128)} %get-tuple-element.50) | copy-start | bytes 3686404
  288.7 9.3 %copy-start.3 = (bf16[120,2048]{1,0:T(8,128)(2,1)S(1)}, bf16[120,2048]{1,0:T(8,128)(2,1)}, u32[]{:S(2)}) copy-start(bf16[120,2048]{1,0:T(8,128)(2,1)} %get-tuple-element.85) | copy-start | bytes 1474564

commit v3 on v2

--- a/solution.py
+++ b/solution.py
@@ -199,10 +199,16 @@
 
     def slot(self, t):
         self.stage(0, t + 2)
-        for stage in (1, 2, 3):
+        for stage in (2, 3, 1):
             self.stage(stage, t - (stage - 1))
+
+        @pl.when(t == 2)
+        def _():
+            self.cores(0)
+
+    def cores(self, slot):
         for lane in self.plan.lanes:
-            lane.at(t - 2, functools.partial(self.core, lane))
+            lane.at(slot, functools.partial(self.core, lane))
 
     def core(self, lane, m):
         if self.grid.C == 2:
@@ -213,6 +219,7 @@
 
     def finish(self):
         def end(t, carry):
+            pl.when(t > 0)(lambda: self.cores(t))
             for stage in range(4):
                 self.stage(stage, t, True)
             return carry

time: 299 us -> 295 us (0.987)
  Pallas kernels: 257 us -> 253 us
    pallas_call x1, Pallas kernels: 120 us -> 115 us  [first_half(): pl.pallas_call(functools.partial(first_kernel, sz, plan, width, row_seque...]
where the time goes in v3:
time: 295 us
  Pallas kernels  253 us (86%)
  matrix products  22.3 us (8%)
  local copies, waits for them, and re-layouts  12.5 us (4%)
  other arithmetic  5.83 us (2%)
    pallas_call x1, Pallas kernels, last_half(): pl.pallas_call(functools.partial(last_kernel, sz, plan, width), out_shape...  139 us
    pallas_call x1, Pallas kernels, first_half(): pl.pallas_call(functools.partial(first_kernel, sz, plan, width, row_seque...  115 us
    dot_general x5, matrix products, einsum(): return jnp.einsum(form, a, b, preferred_element_type=F32)  22.3 us

profile of v3, /device:TPU:0, one launch (start us, length us, event | category | flops | bytes accessed | tf_op | source)
XLA Modules:
  0.0 294.7 jit_solution(1325105670181433113)
XLA Ops:
  0.6 0.7 select_maximum_fusion.1
  1.3 0.7 convert_reduce_fusion
  2.0 0.6 select_maximum_fusion.small_ref
  2.6 0.8 copy.24
  3.5 0.8 copy.25
  4.3 0.9 copy.23
  5.3 2.0 concatenate.10.w_ref
  7.3 114.7 %first_half.1 = (bf16[8,120,256]{2,1,0:T(8,128)(2,1)}, bf16[8,120,256]{2,1,0:T(8,128)(2,1)}, bf16[4,8,120,2560]{3,2,1,0:T(8,128)(2,1)}, bf16[4,8,120,640]{3,2,1,...) custom-call(bf16[120,2048]{1,0:T(8,128)(2,1)} %x_ref.1, ...), custom_call_target="tpu_custom_call" | custom-call | tf_op jit(solution)/shard_map/first_half/pallas_call | solution.py:739
  122.0 4.2 %fusion = f32[4,640,256]{2,1,0:T(8,128)S(1)} fusion(bf16[960,256,1]{1,0,2:T(8,128)(2,1)} %bitcast.44, bf16[4,960,2560]{2,1,0:T(8,128)(2,1)} %bitcast.32), kind=kOutput, calls=%fused_computation.1 | convolution fusion | flops 1258291200 | bytes 8028160 | tf_op jit(solution)/shard_map/jdf,dt->jft/dot_general | solution.py:997
  126.3 4.1 %fusion.4 = f32[4,640,256]{2,1,0:T(8,128)S(1)} fusion(bf16[960,256,1]{1,0,2:T(8,128)(2,1)S(1)} %bitcast.38, bf16[4,960,2560]{2,1,0:T(8,128)(2,1)} %bitcast.33), kind=kOutput, calls=%fused_computation.5 | convolution fusion | flops 1258291200 | bytes 8028160 | tf_op jit(solution)/shard_map/jdf,dt->jft/dot_general | solution.py:997
  130.3 5.0 %multiply_convert_fusion = (bf16[4,640,256]{2,1,0:T(8,128)(2,1)S(1)}, bf16[4,640,256]{2,1,0:T(8,128)(2,1)S(1)}, bf16[4,640,256]{2,1,0:T(8,128)(2,1)S(1)}) fusion(f32[4,640,256]{2,1,0:T(8,128)S(1)} %fusion, f32[4,640,256]{2,1,0:T(8,128)S(1)} %fusion.4, bf16[960,256,1]{1,0,2:T(8,128)(2,1)S(1)} %bitcast.45, bf16[4,960,2560]{2,1,0:T(8,128)(2,1)} %bitcast.34), kind=kOutput, calls=%fused_computation.9 | convolution fusion | flops 1268776960 | bytes 14581760 | tf_op jit(solution)/shard_map/jdf,dt->jft/dot_general | solution.py:997
  135.4 5.4 %convolution_convert_fusion = bf16[4,1280,960]{1,2,0:T(8,128)(2,1)} fusion(bf16[960,256,1]{1,0,2:T(8,128)(2,1)S(1)} %bitcast.46, bf16[4,640,256]{2,1,0:T(8,128)(2,1)S(1)} %get-tuple-element.64, bf16[4,640,256]{2,1,0:T(8,128)(2,1)S(1)} %get-tuple-element.63), kind=kOutput, calls=%fused_computation | convolution fusion | flops 2526740480 | bytes 12943360 | tf_op jit(solution)/shard_map/dt,jft->jdf/dot_general | solution.py:997
  140.7 3.7 %convolution_convert_fusion.1 = bf16[4,640,960]{1,2,0:T(8,128)(2,1)} fusion(bf16[4,640,256]{2,1,0:T(8,128)(2,1)S(1)} %get-tuple-element.62.hidden_ref, bf16[960,256,1]{1,0,2:T(8,128)(2,1)S(1)} %bitcast.39), kind=kOutput, calls=%fused_computation.7 | convolution fusion | flops 1260748800 | bytes 6717440 | tf_op jit(solution)/shard_map/dt,jft->jdf/dot_general | solution.py:997
  144.4 1.6 pad_maximum_fusion.back_ref
  146.1 138.5 %last_half.1 = (bf16[120,2048]{1,0:T(8,128)(2,1)}, bf16[120,2048]{1,0:T(8,128)(2,1)}, f32[120,2560]{1,0:T(8,128)}, f32[8,128]{1,0:T(8,128)}) custom-call(bf16[4,4,2,120,1280]{4,3,2,1,0:T(8,128)(2,1)} %bitcast.37, bf16[4,4,2,120,640]{4,3,2,1,0:T(8,128)(2,1)} %bitcast.36, bf16[4,4,2,120,2560]{4,3,2,1,0:T(8,128)(2,1)} %bitcast.35, ...), custom_call_target="tpu_custom_call" | custom-call | tf_op jit(solution)/shard_map/last_half/pallas_call | solution.py:955
  284.6 2.2 convert_element_type.43
  286.8 1.3 slice_bitcast_fusion.2
  288.1 1.6 slice_bitcast_fusion.1
  289.7 1.1 fusion.6
  290.8 0.7 copy.26
  291.5 0.7 copy.27
  292.2 0.7 copy.28
  293.0 0.9 slice_bitcast_fusion
  293.9 0.8 copy.30
  (11 shorter events, 0.0 us)
Async XLA Ops:
  122.0 4.2 %copy-start.1 = (bf16[8,120,256]{2,1,0:T(8,128)(2,1)S(1)}, bf16[8,120,256]{2,1,0:T(8,128)(2,1)}, u32[]{:S(2)}) copy-start(bf16[8,120,256]{2,1,0:T(8,128)(2,1)} %get-tuple-element.32.dy_ref) | copy-start | bytes 1474564
  126.3 4.1 %copy-start.4 = (bf16[8,120,256]{2,1,0:T(8,128)(2,1)S(1)}, bf16[8,120,256]{2,1,0:T(8,128)(2,1)}, u32[]{:S(2)}) copy-start(bf16[8,120,256]{2,1,0:T(8,128)(2,1)} %get-tuple-element.33) | copy-start | bytes 1474564
  135.4 5.4 %copy-start = (bf16[4,640,256]{2,1,0:T(8,128)(2,1)}, bf16[4,640,256]{2,1,0:T(8,128)(2,1)S(1)}, u32[]{:S(2)}) copy-start(bf16[4,640,256]{2,1,0:T(8,128)(2,1)S(1)} %get-tuple-element.62.hidden_ref) | copy-start | bytes 3932164
  284.6 8.3 %copy-start.2 = (f32[120,2560]{1,0:T(8,128)S(1)}, f32[120,2560]{1,0:T(8,128)}, u32[]{:S(2)}) copy-start(f32[120,2560]{1,0:T(8,128)} %get-tuple-element.50) | copy-start | bytes 3686404
  284.6 9.3 %copy-start.3 = (bf16[120,2048]{1,0:T(8,128)(2,1)S(1)}, bf16[120,2048]{1,0:T(8,128)(2,1)}, u32[]{:S(2)}) copy-start(bf16[120,2048]{1,0:T(8,128)(2,1)} %get-tuple-element.85) | copy-start | bytes 1474564

commit v4 on v3

--- a/solution.py
+++ b/solution.py
@@ -1038,11 +1038,11 @@
     ) = first_half(sz, row_tokens // PACKED_LENGTH, block_input, out_cotangent, small, block)
     dy_half = dy_parts.reshape(features, tok)
     w_cols = w_all.reshape(GY, features, -1)
-    w_gate, w_up, w_down = (w_cols[:, :, k * width : k * width + fc] for k in range(1, 4))
+    w_down = w_cols[:, :, 3 * width : 3 * width + fc]
     normed_two = normed_two.reshape(features, tok)
 
-    gate = einsum("jdf,dt->jft", w_gate, normed_two)
-    up = einsum("jdf,dt->jft", w_up, normed_two)
+    gate_up = einsum("jdf,dt->jft", w_cols[:, :, width : 3 * width], normed_two)
+    gate, up = gate_up[:, :fc], gate_up[:, width : width + fc]
     sigmoid = jax.nn.sigmoid(gate)
     hidden = padded((jax.nn.silu(gate) * up).astype(BF16), 1, width)
     hidden_grad = einsum("jdf,dt->jft", w_down, dy_half)

time: 295 us -> 293 us (level)
    dot_general x5 -> x4, matrix products: 22.3 us -> 19.8 us  [einsum(): return jnp.einsum(form, a, b, preferred_element_type=F32)]
where the time goes in v4:
time: 293 us; the launch traced here: 292 us
  Pallas kernels  253 us (86%)
  matrix products  19.8 us (7%)
  local copies, waits for them, and re-layouts  12.5 us (4%)
  other arithmetic  5.83 us (2%)
    pallas_call x1, Pallas kernels, last_half(): pl.pallas_call(functools.partial(last_kernel, sz, plan, width), out_shape...  139 us
    pallas_call x1, Pallas kernels, first_half(): pl.pallas_call(functools.partial(first_kernel, sz, plan, width, row_seque...  115 us
    dot_general x4, matrix products, einsum(): return jnp.einsum(form, a, b, preferred_element_type=F32)  19.8 us

profile of v4, /device:TPU:0, one launch (start us, length us, event | category | flops | bytes accessed | tf_op | source)
XLA Modules:
  0.0 292.1 jit_solution(9794538230133472727)
XLA Ops:
  0.6 0.7 select_maximum_fusion.1
  1.3 0.7 convert_reduce_fusion
  2.0 0.6 select_maximum_fusion.small_ref
  2.6 0.8 copy.24
  3.5 0.8 copy.25
  4.3 0.9 copy.23
  5.3 2.0 concatenate.10.w_ref
  7.3 114.7 %first_half.1 = (bf16[8,120,256]{2,1,0:T(8,128)(2,1)}, bf16[8,120,256]{2,1,0:T(8,128)(2,1)}, bf16[4,8,120,2560]{3,2,1,0:T(8,128)(2,1)}, bf16[4,8,120,640]{3,2,1,...) custom-call(bf16[120,2048]{1,0:T(8,128)(2,1)} %x_ref.1, ...), custom_call_target="tpu_custom_call" | custom-call | tf_op jit(solution)/shard_map/first_half/pallas_call | solution.py:739
  122.0 5.8 %fusion = f32[4,1280,256]{2,1,0:T(8,128)S(1)} fusion(bf16[960,256,1]{1,0,2:T(8,128)(2,1)} %bitcast.42, bf16[4,960,2560]{2,1,0:T(8,128)(2,1)} %bitcast.31), kind=kOutput, calls=%fused_computation.1 | convolution fusion | flops 2516582400 | bytes 15564800 | tf_op jit(solution)/shard_map/jdf,dt->jft/dot_general | solution.py:997
  127.9 5.1 %multiply_convert_fusion.2 = (bf16[4,640,256]{2,1,0:T(8,128)(2,1)S(1)}, bf16[4,640,256]{2,1,0:T(8,128)(2,1)S(1)}, bf16[4,640,256]{2,1,0:T(8,128)(2,1)S(1)}) fusion(f32[4,1280,256]{2,1,0:T(8,128)S(1)} %fusion, bf16[960,256,1]{1,0,2:T(8,128)(2,1)S(1)} %bitcast.36, bf16[4,960,2560]{2,1,0:T(8,128)(2,1)} %bitcast.32), kind=kOutput, calls=%fused_computation.9 | convolution fusion | flops 1268776960 | bytes 14581760 | tf_op jit(solution)/shard_map/jdf,dt->jft/dot_general | solution.py:997
  133.0 5.2 %convolution_convert_fusion = bf16[4,1280,960]{1,2,0:T(8,128)(2,1)} fusion(bf16[960,256,1]{1,0,2:T(8,128)(2,1)S(1)} %bitcast.43, bf16[4,640,256]{2,1,0:T(8,128)(2,1)S(1)} %get-tuple-element.63, bf16[4,640,256]{2,1,0:T(8,128)(2,1)S(1)} %get-tuple-element.62), kind=kOutput, calls=%fused_computation | convolution fusion | flops 2526740480 | bytes 12943360 | tf_op jit(solution)/shard_map/dt,jft->jdf/dot_general | solution.py:997
  138.2 0.0 copy-done
  138.2 3.7 %convolution_convert_fusion.1 = bf16[4,640,960]{1,2,0:T(8,128)(2,1)} fusion(bf16[4,640,256]{2,1,0:T(8,128)(2,1)S(1)} %get-tuple-element.64.hidden_ref, bf16[960,256,1]{1,0,2:T(8,128)(2,1)S(1)} %bitcast.37), kind=kOutput, calls=%fused_computation.5 | convolution fusion | flops 1260748800 | bytes 6717440 | tf_op jit(solution)/shard_map/dt,jft->jdf/dot_general | solution.py:997
  141.9 1.6 pad_maximum_fusion.back_ref
  143.5 138.5 %last_half.1 = (bf16[120,2048]{1,0:T(8,128)(2,1)}, bf16[120,2048]{1,0:T(8,128)(2,1)}, f32[120,2560]{1,0:T(8,128)}, f32[8,128]{1,0:T(8,128)}) custom-call(bf16[4,4,2,120,1280]{4,3,2,1,0:T(8,128)(2,1)} %bitcast.35, bf16[4,4,2,120,640]{4,3,2,1,0:T(8,128)(2,1)} %bitcast.34, bf16[4,4,2,120,2560]{4,3,2,1,0:T(8,128)(2,1)} %bitcast.33, ...), custom_call_target="tpu_custom_call" | custom-call | tf_op jit(solution)/shard_map/last_half/pallas_call | solution.py:955
  282.1 2.2 convert_element_type.43
  284.3 1.3 slice_bitcast_fusion.2
  285.6 1.6 slice_bitcast_fusion.1
  287.2 1.1 fusion.4
  288.2 0.7 copy.26
  289.0 0.7 copy.27
  289.7 0.7 copy.28
  290.4 0.9 slice_bitcast_fusion
  291.4 0.8 copy.30
  (10 shorter events, 0.0 us)
Async XLA Ops:
  122.0 5.9 %copy-start.1 = (bf16[8,120,256]{2,1,0:T(8,128)(2,1)S(1)}, bf16[8,120,256]{2,1,0:T(8,128)(2,1)}, u32[]{:S(2)}) copy-start(bf16[8,120,256]{2,1,0:T(8,128)(2,1)} %get-tuple-element.32.dy_ref) | copy-start | bytes 1474564
  127.9 5.1 %copy-start.4 = (bf16[8,120,256]{2,1,0:T(8,128)(2,1)S(1)}, bf16[8,120,256]{2,1,0:T(8,128)(2,1)}, u32[]{:S(2)}) copy-start(bf16[8,120,256]{2,1,0:T(8,128)(2,1)} %get-tuple-element.33) | copy-start | bytes 1474564
  133.0 5.2 %copy-start = (bf16[4,640,256]{2,1,0:T(8,128)(2,1)}, bf16[4,640,256]{2,1,0:T(8,128)(2,1)S(1)}, u32[]{:S(2)}) copy-start(bf16[4,640,256]{2,1,0:T(8,128)(2,1)S(1)} %get-tuple-element.64.hidden_ref) | copy-start | bytes 3932164
  282.1 8.3 %copy-start.2 = (f32[120,2560]{1,0:T(8,128)S(1)}, f32[120,2560]{1,0:T(8,128)}, u32[]{:S(2)}) copy-start(f32[120,2560]{1,0:T(8,128)} %get-tuple-element.50) | copy-start | bytes 3686404
  282.1 9.3 %copy-start.3 = (bf16[120,2048]{1,0:T(8,128)(2,1)S(1)}, bf16[120,2048]{1,0:T(8,128)(2,1)}, u32[]{:S(2)}) copy-start(bf16[120,2048]{1,0:T(8,128)(2,1)} %get-tuple-element.85) | copy-start | bytes 1474564
